TPU v7x, 32 devices: a whole 2x2x4 slice. The times are simulated.
32 devices in a mesh: group: 8 (over z, y), tok: 4 (over x, core).
Axes of the slice: x: 2, y: 2, z: 4, core: 2. Of those that a mesh axis runs over, the one named last changes fastest.
Arguments:
- tokens: bfloat16 [16384, 2048], P(('group', 'tok')), may hold values from -94 to 94
- learning_rates: float32 [2, 16384], P(None, 'group'), may hold values from 0.1 to 1
- channel_gains: float32 [2, 5, 2048], P(None, None, 'tok'), may hold values from 0.3 to 3
- fast_init: float32 [2, 3, 16, 128, 128], P(None, None, 'tok'), may hold values from -0.5 to 0.5
- step_size: float32 [2, 16], P(None, 'tok'), may hold values from 0.05 to 1
- update_table: int32 [2, 8], replicated, may hold values 0 or 1
Outputs:
- mixed: bfloat16 [16384, 2048], P(('group', 'tok'))
All inputs are finite; a program needn't handle non-finite values.
Results may differ from a plain program's by a relative error of at most 0.033.
Values may be sent and summed in bfloat16 or wider, within the bound.
A program may use at most 64 MiB of HBM per device.

v0:
```python
import functools

import jax
import jax.numpy as jnp
from jax import lax
from jax.experimental import pallas as pl
from jax.experimental.pallas import tpu as pltpu
from jax.sharding import PartitionSpec as P

NS_STEPS = 5


MUON_A = 3.4445
MUON_B = -4.775
MUON_C = 2.0315
EPSILON = 1e-06


def passed_along(value, axis, by):
    size = lax.axis_size(axis)
    pairs = [(i, i + by) for i in range(size) if 0 <= i + by < size]
    return lax.ppermute(value, axis, pairs)


def orthogonalize(gradient):
    scaling = lax.rsqrt(jnp.sum(gradient * gradient, axis=(-2, -1), keepdims=True) + EPSILON)
    current = gradient * scaling
    for repeat in range(NS_STEPS):
        square = jnp.einsum("...ij,...kj->...ik", current, current, precision=lax.Precision.HIGHEST)
        polynom = MUON_B * square + MUON_C * jnp.einsum(
            "...ij,...jk->...ik", square, square, precision=lax.Precision.HIGHEST
        )
        current = MUON_A * current + jnp.einsum(
            "...ij,...jk->...ik", polynom, current, precision=lax.Precision.HIGHEST
        )
    return current


def layer_group(stream, entering, gain_rows, rates_row, steps_row, update_flag, inverse):
    row_count, channel_count = stream.shape
    heads_n = entering.shape[1]
    head_dim = entering.shape[2]
    normed = stream.astype(jnp.float32) * inverse[:, None] * gain_rows[0]
    queries = (normed * gain_rows[1]).astype(jnp.bfloat16).reshape(row_count, heads_n, head_dim)
    keys_in = (normed * gain_rows[2]).astype(jnp.bfloat16).reshape(row_count, heads_n, head_dim)
    values_in = (normed * gain_rows[3]).astype(jnp.bfloat16).reshape(row_count, heads_n, head_dim)
    rounded = entering.astype(jnp.bfloat16)
    gate_q = jnp.einsum("thi,hij->thj", queries, rounded[0], preferred_element_type=jnp.float32)
    up_q = jnp.einsum("thi,hij->thj", queries, rounded[1], preferred_element_type=jnp.float32)
    hidden_q = (jax.nn.silu(gate_q) * up_q).astype(jnp.bfloat16)
    output = jnp.einsum(
        "thj,hjk->thk", hidden_q, rounded[2], preferred_element_type=jnp.float32
    ).reshape(row_count, channel_count)
    mixed_rows = (stream.astype(jnp.float32) + gain_rows[4] * output).astype(jnp.bfloat16)
    gate_k = jnp.einsum("thi,hij->thj", keys_in, rounded[0], preferred_element_type=jnp.float32)
    up_k = jnp.einsum("thi,hij->thj", keys_in, rounded[1], preferred_element_type=jnp.float32)
    sigmoid_k = jax.nn.sigmoid(gate_k)
    active_k = gate_k * sigmoid_k
    hidden_k = (active_k * up_k).astype(jnp.bfloat16)
    targets = (rates_row[:, None, None] * values_in.astype(jnp.float32)).astype(jnp.bfloat16)
    back_hidden = jnp.einsum(
        "thk,hjk->thj", targets, rounded[2], preferred_element_type=jnp.float32
    )
    back_up = (back_hidden * active_k).astype(jnp.bfloat16)
    back_gate = (back_hidden * up_k * sigmoid_k * (1.0 + gate_k * (1.0 - sigmoid_k))).astype(
        jnp.bfloat16
    )
    grad_gate = jnp.einsum("thi,thj->hij", keys_in, back_gate, preferred_element_type=jnp.float32)
    grad_up = jnp.einsum("thi,thj->hij", keys_in, back_up, preferred_element_type=jnp.float32)
    grad_down = jnp.einsum("thj,thk->hjk", hidden_k, targets, preferred_element_type=jnp.float32)
    direction = orthogonalize(jnp.stack([grad_gate, grad_up, grad_down]))
    moved_state = entering + (update_flag * steps_row)[None, :, None, None] * direction
    norm_before = jnp.sqrt(jnp.sum(entering * entering, axis=2, keepdims=True) + EPSILON)
    norm_after = jnp.sqrt(jnp.sum(moved_state * moved_state, axis=2, keepdims=True) + EPSILON)
    return (mixed_rows, moved_state * (norm_before / norm_after))


def pass_on(outgoing):
    return passed_along(outgoing, "group", 1)


def body(tokens, learning_rates, channel_gains, fast_init, step_size, update_table):
    start_stream = lax.all_to_all(tokens, "tok", split_axis=1, concat_axis=0, tiled=True)
    group_count = lax.axis_size("group")
    group_index = lax.axis_index("group")
    width_all = start_stream.shape[1] * lax.axis_size("tok")
    layer_count = fast_init.shape[0]
    zero_state = jnp.zeros(fast_init.shape[1:], jnp.float32)

    def tick_work(stream, outgoing, layer_now, active, inverse):
        received = pass_on(outgoing)
        initial = lax.dynamic_index_in_dim(fast_init, layer_now, 0, keepdims=False)
        entering = jnp.where(group_index == 0, initial, received)
        gain_rows = lax.dynamic_index_in_dim(channel_gains, layer_now, 0, keepdims=False)
        rates_row = lax.dynamic_index_in_dim(learning_rates, layer_now, 0, keepdims=False)
        steps_row = lax.dynamic_index_in_dim(step_size, layer_now, 0, keepdims=False)
        table_cell = lax.dynamic_slice(
            update_table, (jnp.asarray(layer_now, jnp.int32), group_index), (1, 1)
        )
        update_flag = table_cell[0, 0].astype(jnp.float32)

        def working(operands):
            return layer_group(
                operands[0], operands[1], gain_rows, rates_row, steps_row, update_flag, inverse
            )

        def resting(operands):
            return (operands[0], operands[2])

        return lax.cond(active, working, resting, (stream, entering, outgoing))

    def one_tick(tick_index, loop_state):
        stream, outgoing = loop_state
        layer_raw = tick_index - group_index
        active = (layer_raw >= 0) & (layer_raw < layer_count)
        layer_now = jnp.clip(layer_raw, 0, layer_count - 1)
        widened = stream.astype(jnp.float32)
        totals = lax.psum(jnp.sum(widened * widened, axis=1), "tok")
        inverse = lax.rsqrt(totals / width_all + EPSILON)
        return tick_work(stream, outgoing, layer_now, active, inverse)

    final_stream, last_state = lax.fori_loop(
        0, layer_count + group_count - 1, one_tick, (start_stream, zero_state)
    )
    return lax.all_to_all(final_stream, "tok", split_axis=0, concat_axis=1, tiled=True)


MESH = pl.DeviceIdType.MESH
F32 = jnp.float32
BF16 = jnp.bfloat16
NN = (((1,), (0,)), ((), ()))
NT = (((1,), (1,)), ((), ()))
TN = (((0,), (0,)), ((), ()))


def dot(a, b, dims=NN):
    return lax.dot_general(a, b, dims, preferred_element_type=F32)


def halves(value):
    high = value.astype(BF16)
    return high, (value - high.astype(F32)).astype(BF16)


def product(a, b):
    a_high, a_low = halves(a)
    b_high, b_low = halves(b)
    left = jnp.concatenate([a_high, a_low], axis=1)
    above = jnp.concatenate([b_high, b_low], axis=1)
    below = jnp.concatenate([b_high, jnp.zeros_like(b_low)], axis=1)
    both = dot(left, jnp.concatenate([above, below], axis=0))
    return both[:, : b.shape[1]] + both[:, b.shape[1] :]


def gram(a):
    high, low = halves(a)
    left = jnp.concatenate([high, low], axis=1)
    above = jnp.concatenate([high, high], axis=1)
    below = jnp.concatenate([low, jnp.zeros_like(low)], axis=1)
    both = dot(left, jnp.concatenate([above, below], axis=0), NT)
    return both[:, : a.shape[0]] + both[:, a.shape[0] :]


def sigmoid(value):
    return 0.5 * jnp.tanh(0.5 * value) + 0.5


def newton_schulz(values):
    squares = [gram(v) for v in values]
    polynoms = [MUON_B * q + MUON_C * product(q, q) for q in squares]
    return tuple(MUON_A * v + product(p, v) for p, v in zip(polynoms, values))


def chain_kernel(
    sizes,
    tokens,
    rates,
    packed,
    flags,
    initial,
    out,
    xin,
    xout,
    squares,
    sent_squares,
    rate_rows,
    params,
    state,
    totals,
    stack,
    gate_up,
    down,
    grad_gu,
    grad_d,
    x_recv,
    x_send,
    sq_recv,
    sq_send,
    rate_recv,
    rate_send,
    w_recv,
    w_send,
    p_recv,
    p_send,
    t_send,
    s_send,
    out_recv,
):
    groups, toks, layers, heads, owned, rows, width, tile = sizes
    group_tok = rows * toks
    per = toks // layers
    tiles = group_tok // tile
    tiles_row = rows // tile
    g = lax.axis_index("group")
    t = lax.axis_index("tok")
    me = g * toks + t
    layer = lax.rem(t, layers)
    head = g * per + t // layers
    devices = groups * toks

    def remote(source, target, send, recv, to_g, to_t):
        return pltpu.make_async_remote_copy(
            src_ref=source,
            dst_ref=target,
            send_sem=send,
            recv_sem=recv,
            device_id=(to_g, to_t),
            device_id_type=MESH,
        )

    def deliver(source, target, send, recv, to_g, to_t):
        own = to_g * toks + to_t == me

        @pl.when(own)
        def _():
            pltpu.make_async_copy(source, target, recv).start()

        @pl.when(jnp.logical_not(own))
        def _():
            remote(source, target, send, recv, to_g, to_t).start()

    def sent(source, send, to_g, to_t):
        @pl.when(to_g * toks + to_t != me)
        def _():
            pltpu.make_async_copy(source, source, send).wait()

    def arrived(target, recv):
        pltpu.make_async_copy(target, target, recv).wait()

    barrier = pltpu.get_barrier_semaphore()

    @pl.loop(1, devices)
    def _(step):
        peer = lax.rem(me + step, devices)
        pl.semaphore_signal(
            barrier, inc=1, device_id=(peer // toks, lax.rem(peer, toks)), device_id_type=MESH
        )

    pl.semaphore_wait(barrier, devices - 1)

    def lane(index, size):
        return pl.ds(pl.multiple_of(index * size, size), size)

    def param_of(to_t):
        wanted = g * per + to_t // layers
        return wanted // owned == t, lax.rem(to_t, layers), lax.rem(wanted, owned)

    for to_t in range(toks):
        holds, lay, slot = param_of(to_t)

        @pl.when(holds)
        def _():
            deliver(initial.at[lay, :, slot], state, w_send.at[to_t], w_recv, g, to_t)
            deliver(packed.at[lay, slot], params, p_send.at[to_t], p_recv, g, to_t)

    @pl.loop(0, groups)
    def _(i):
        to_g = lax.rem(g + i, groups)
        deliver(rates.at[layer], rate_rows.at[g], rate_send.at[to_g], rate_recv, to_g, t)

    @pl.loop(0, heads)
    def _(i):
        h = lax.rem(head + i, heads)
        to_g, to_t = h // per, lax.rem(h, per) * layers
        deliver(
            tokens.at[:, lane(h, width)],
            xin.at[lane(g * toks + t, rows)],
            t_send.at[h],
            x_recv.at[g, t],
            to_g,
            to_t,
        )

    ones_rows = jnp.ones((16, width), BF16)

    def sums_of(values):
        wide = values.astype(F32)
        return dot(ones_rows, (wide * wide).astype(BF16), NT)[0:1]

    totals[...] = jnp.zeros_like(totals)

    @pl.loop(0, heads)
    def _(h):
        totals[...] += sums_of(tokens[:, lane(h, width)])

    @pl.loop(0, heads)
    def _(i):
        h = lax.rem(head + i, heads)
        to_g, to_t = h // per, lax.rem(h, per) * layers
        deliver(
            totals, squares.at[g, 0, :, lane(t, rows)], s_send.at[h], sq_recv.at[g], to_g, to_t
        )

    arrived(state, w_recv)
    arrived(params, p_recv)
    arrived(rate_rows, rate_recv)

    gains = params[...]
    norm_gain = gains[0:1]
    query_gain = norm_gain * gains[1:2]
    key_gain = norm_gain * gains[2:3]
    value_gain = norm_gain * gains[3:4]
    out_gain = gains[4:5]
    step_row = gains[5:6]
    pick_row = lax.broadcasted_iota(jnp.int32, (16, 2 * width), 0)
    pick_lane = lax.broadcasted_iota(jnp.int32, (16, 2 * width), 1)
    spread = jnp.where(pick_row // 2 == pick_lane // width, 1.0, 0.0).astype(BF16)
    @pl.loop(0, groups)
    def _(c):
        whole = squares.at[c]

        @pl.when(layer == 0)
        def _():
            arrived(squares.at[c, 0], sq_recv.at[c])
            sent_squares[c] = squares[c, 0]

        @pl.when(layer > 0)
        def _():
            arrived(whole, sq_recv.at[c])
            sent_squares[c] = jnp.sum(squares[c], axis=0)

        inverse = lax.rsqrt(sent_squares[c] / (heads * width) + EPSILON)
        rate = rate_rows[c]
        inverse_high = inverse.astype(BF16).astype(F32)
        rate_high = rate.astype(BF16).astype(F32)
        at_row = lax.broadcasted_iota(jnp.int32, (16, group_tok), 0)
        fill = jnp.where(at_row == 0, inverse_high, 0.0)
        fill = jnp.where(at_row == 1, inverse - inverse_high, fill)
        fill = jnp.where(at_row == 2, rate_high, fill)
        stack[...] = jnp.where(at_row == 3, rate - rate_high, fill).astype(BF16)

        gate_up[:, :width] = state[0].astype(BF16)
        gate_up[:, width:] = state[1].astype(BF16)
        down[...] = state[2].astype(BF16)

        def read(i):
            at = lane(c * tiles + i, tile)
            here = lane(i, tile)

            def query():
                stream = xin[at, :].astype(F32)
                normed = stream * dot(stack[:, here], spread[:, :width], TN)
                queries = (normed * query_gain).astype(BF16)
                both = dot(queries, gate_up[...])
                gate = both[:, :width]
                hidden = (gate * sigmoid(gate) * both[:, width:]).astype(BF16)
                mixed = (stream + out_gain * dot(hidden, down[...])).astype(BF16)
                xout[at, :] = mixed
                sent_squares[c, :, here] = sums_of(mixed)

            def learn():
                scale = dot(stack[:, here], spread, TN)
                normed = xin[at, :].astype(F32) * scale[:, :width]
                keys = (normed * key_gain).astype(BF16)
                targets = (normed * value_gain * scale[:, width:]).astype(BF16)
                both = dot(keys, gate_up[...])
                back = dot(targets, down[...], NT)
                gate = both[:, :width]
                up = both[:, width:]
                sig = sigmoid(gate)
                act = gate * sig
                hidden = (act * up).astype(BF16)
                back_up = (back * act).astype(BF16)
                back_gate = (back * up * (sig + act * (1.0 - sig))).astype(BF16)
                backs = jnp.concatenate([back_gate, back_up], axis=1)
                return dot(keys, backs, TN), dot(hidden, targets, TN)

            return query, learn

        def answer(k):
            for i in range(tiles_row):
                read(k * tiles_row + i)[0]()

        def await_rows(k):
            arrived(xin.at[lane(c * toks + k, rows)], x_recv.at[c, k])

        def send_rows(k):
            block = xout.at[lane(c * toks + k, rows)]

            @pl.when(layer < layers - 1)
            def _():
                remote(
                    block,
                    xin.at[lane(c * toks + k, rows)],
                    x_send.at[c, k],
                    x_recv.at[c, k],
                    g,
                    t + 1,
                ).start()

            @pl.when(layer == layers - 1)
            def _():
                deliver(block, out.at[:, lane(head, width)], x_send.at[c, k], out_recv, c, k)

        def send_squares():
            @pl.when(layer < layers - 1)
            def _():
                @pl.loop(0, heads)
                def _(h):
                    remote(
                        sent_squares.at[c],
                        squares.at[c, head],
                        sq_send.at[c],
                        sq_recv.at[c],
                        h // per,
                        lax.rem(h, per) * layers + layer + 1,
                    ).start()

        @pl.when(c == groups - 1)
        def _():
            @pl.loop(0, toks)
            def _(k):
                await_rows(k)
                answer(k)
                send_rows(k)

            send_squares()

        @pl.when(c < groups - 1)
        def _():
            grad_gu[...] = jnp.zeros_like(grad_gu)
            grad_d[...] = jnp.zeros_like(grad_d)

            @pl.loop(0, toks)
            def _(k):
                await_rows(k)
                found = [read(k * tiles_row + i)[1]() for i in range(tiles_row)]
                grad_gu[...] += sum(f[0] for f in found)
                grad_d[...] += sum(f[1] for f in found)

            grads = (grad_gu[:, :width], grad_gu[:, width:], grad_d[...])
            start = tuple(
                v * lax.rsqrt(jnp.sum(v * v, axis=(0, 1), keepdims=True) + EPSILON) for v in grads
            )

            def beside(k, values):
                answer(k)
                values = newton_schulz(values)
                send_rows(k)
                return values

            moves = lax.fori_loop(0, toks, beside, start)
            send_squares()
            for _ in range(NS_STEPS - toks):
                moves = newton_schulz(moves)
            step = step_row * flags[c]
            for which in range(3):
                entering = state[which]
                moved = entering + step * moves[which]
                before = jnp.sum(entering * entering, axis=0, keepdims=True) + EPSILON
                after = jnp.sum(moved * moved, axis=0, keepdims=True) + EPSILON
                state[which] = moved * (jnp.sqrt(before) * lax.rsqrt(after))

    arrived(out, out_recv)

    for to_t in range(toks):
        holds, lay, slot = param_of(to_t)

        @pl.when(holds)
        def _():
            sent(initial.at[lay, :, slot], w_send.at[to_t], g, to_t)
            sent(packed.at[lay, slot], p_send.at[to_t], g, to_t)

    @pl.loop(0, groups)
    def _(to_g):
        sent(rates.at[layer], rate_send.at[to_g], to_g, t)

        @pl.when(layer < layers - 1)
        def _():
            arrived(squares.at[to_g], sq_send.at[to_g])

        @pl.loop(0, toks)
        def _(k):
            block = xout.at[lane(to_g * toks + k, rows)]

            @pl.when(layer < layers - 1)
            def _():
                arrived(block, x_send.at[to_g, k])

            @pl.when(layer == layers - 1)
            def _():
                sent(block, x_send.at[to_g, k], to_g, k)

    @pl.loop(0, heads)
    def _(h):
        to_g, to_t = h // per, lax.rem(h, per) * layers
        sent(totals, s_send.at[h], to_g, to_t)
        sent(tokens.at[:, lane(h, width)], t_send.at[h], to_g, to_t)


def head_body(tokens, learning_rates, channel_gains, fast_init, step_size, update_table):
    groups, toks = lax.axis_size("group"), lax.axis_size("tok")
    layers, _, owned, width, _ = fast_init.shape
    rows, channels = tokens.shape
    heads = owned * toks
    group_tok = rows * toks
    rates = learning_rates.reshape(layers, 1, group_tok)
    gains = channel_gains.reshape(layers, 5, owned, width).transpose(0, 2, 1, 3)
    steps = jnp.broadcast_to(step_size[:, :, None, None], (layers, owned, 3, width))
    packed = jnp.concatenate([gains, steps], axis=2)
    layer = lax.rem(lax.axis_index("tok"), layers)
    flag_row = lax.dynamic_index_in_dim(update_table, layer, 0, keepdims=False).astype(F32)
    flags = jnp.broadcast_to(flag_row[:, None, None], (groups, 1, width))
    tile = 512
    sizes = (groups, toks, layers, heads, owned, rows, width, tile)
    vmem = pl.BlockSpec(memory_space=pltpu.VMEM)
    anywhere = pl.BlockSpec(memory_space=pl.ANY)
    dma = pltpu.SemaphoreType.DMA
    return pl.pallas_call(
        functools.partial(chain_kernel, sizes),
        out_shape=jax.ShapeDtypeStruct((rows, channels), BF16),
        in_specs=[vmem, vmem, vmem, vmem, anywhere],
        out_specs=anywhere,
        scratch_shapes=[
            pltpu.VMEM((groups * group_tok, width), BF16),
            pltpu.VMEM((groups * group_tok, width), BF16),
            pltpu.VMEM((groups, heads, 1, group_tok), F32),
            pltpu.VMEM((groups, 1, group_tok), F32),
            pltpu.VMEM((groups, 1, group_tok), F32),
            pltpu.VMEM((8, width), F32),
            pltpu.VMEM((3, width, width), F32),
            pltpu.VMEM((1, rows), F32),
            pltpu.VMEM((16, group_tok), BF16),
            pltpu.VMEM((width, 2 * width), BF16),
            pltpu.VMEM((width, width), BF16),
            pltpu.VMEM((width, 2 * width), F32),
            pltpu.VMEM((width, width), F32),
            dma((groups, toks)),
            dma((groups, toks)),
            dma((groups,)),
            dma((groups,)),
            dma,
            dma((groups,)),
            dma,
            dma((toks,)),
            dma,
            dma((toks,)),
            dma((heads,)),
            dma((heads,)),
            dma,
        ],
        compiler_params=pltpu.CompilerParams(
            collective_id=0, has_side_effects=True, vmem_limit_bytes=48 * 1024 * 1024
        ),
    )(tokens, rates, packed, flags, fast_init)


def plan(mesh, tokens, fast_init):
    groups, toks = mesh.shape["group"], mesh.shape["tok"]
    layers, _, heads, width, _ = fast_init.shape
    rows = tokens.shape[0] // (groups * toks)
    fits = groups * toks == layers * heads and toks % layers == 0 and heads % toks == 0
    fits = fits and toks <= NS_STEPS and rows % 512 == 0 and width % 128 == 0
    return head_body if fits and tokens.shape[0] * width <= 4 * 1024 * 1024 else body


def solution(mesh):
    in_specs = (
        P(("group", "tok"), None),
        P(None, "group"),
        P(None, None, "tok"),
        P(None, None, "tok", None, None),
        P(None, "tok"),
        P(),
    )
    out_specs = P(("group", "tok"), None)
    def run(*args):
        chosen = plan(mesh, args[0], args[3])
        return jax.shard_map(
            chosen, mesh=mesh, in_specs=in_specs, out_specs=out_specs, check_vma=False
        )(*args)

    return run
```

profile of v0, /device:TPU:29, one launch (start us, length us, event | category | flops | bytes accessed | tf_op | source)
XLA Modules:
  0.0 170.4 jit_solution(15588069629654314759)
XLA Ops:
  0.0 0.7 convert_bitcast_fusion
  0.7 0.1 broadcast_in_dim.5.flags
  0.8 0.7 reshape.15.rates
  1.5 0.8 broadcast_in_dim.4
  2.2 0.8 reshape.16
  3.0 0.0 copy-start
  3.1 1.6 copy-done
  4.6 0.0 copy-start.1
  4.6 1.4 copy-done.1
  6.0 163.0 %shard_map.64 = bf16[512,2048]{1,0:T(8,128)(2,1)S(1)} custom-call(bf16[512,2048]{1,0:T(8,128)(2,1)S(1)} %copy-done, f32[2,1,2048]{2,1,0:T(1,128)S(1)} %reshape.15.rates, f32[2,4,8,128]{3,2,1,0:T(8,128)S(1)} %pad_maximum_fusion.packed, f32[8,1,128]{2,1,0:T(1,128)S(1)} %broadcast_in_dim.5.flags, f32[2,3,4,128,128]{4,3,2,1,0:T(8,128)S(1)} %copy-done.1), custom_call_target="tpu_custom_call" | custom-call | tf_op jit(solution)/shard_map/pallas_call | solution.py:529
  169.1 1.3 copy.11
  (2 shorter events, 0.0 us)
Async XLA Ops:
  3.0 1.6 copy-start
  4.6 1.4 copy-start.1
where the time goes:
time: 173 us; the launch traced here: 170 us
  Pallas kernels  163 us (94%)
  local copies, waits for them, and re-layouts  6.64 us (4%)
    pallas_call x1, Pallas kernels, head_body(): pl.pallas_call(functools.partial(chain_kernel, sizes), out_shape=jax.Shap...  163 us
    unnamed x5, local copies, waits for them, and re-layouts  4.32 us

commit v1 on v0

v1 whole, which is shorter than its diff:
```python
import functools

import jax
import jax.numpy as jnp
from jax import lax
from jax.experimental import pallas as pl
from jax.experimental.pallas import tpu as pltpu
from jax.sharding import PartitionSpec as P

NS_STEPS = 5


MUON_A = 3.4445
MUON_B = -4.775
MUON_C = 2.0315
EPSILON = 1e-06


def passed_along(value, axis, by):
    size = lax.axis_size(axis)
    pairs = [(i, i + by) for i in range(size) if 0 <= i + by < size]
    return lax.ppermute(value, axis, pairs)


def orthogonalize(gradient):
    scaling = lax.rsqrt(jnp.sum(gradient * gradient, axis=(-2, -1), keepdims=True) + EPSILON)
    current = gradient * scaling
    for repeat in range(NS_STEPS):
        square = jnp.einsum("...ij,...kj->...ik", current, current, precision=lax.Precision.HIGHEST)
        polynom = MUON_B * square + MUON_C * jnp.einsum(
            "...ij,...jk->...ik", square, square, precision=lax.Precision.HIGHEST
        )
        current = MUON_A * current + jnp.einsum(
            "...ij,...jk->...ik", polynom, current, precision=lax.Precision.HIGHEST
        )
    return current


def layer_group(stream, entering, gain_rows, rates_row, steps_row, update_flag, inverse):
    row_count, channel_count = stream.shape
    heads_n = entering.shape[1]
    head_dim = entering.shape[2]
    normed = stream.astype(jnp.float32) * inverse[:, None] * gain_rows[0]
    queries = (normed * gain_rows[1]).astype(jnp.bfloat16).reshape(row_count, heads_n, head_dim)
    keys_in = (normed * gain_rows[2]).astype(jnp.bfloat16).reshape(row_count, heads_n, head_dim)
    values_in = (normed * gain_rows[3]).astype(jnp.bfloat16).reshape(row_count, heads_n, head_dim)
    rounded = entering.astype(jnp.bfloat16)
    gate_q = jnp.einsum("thi,hij->thj", queries, rounded[0], preferred_element_type=jnp.float32)
    up_q = jnp.einsum("thi,hij->thj", queries, rounded[1], preferred_element_type=jnp.float32)
    hidden_q = (jax.nn.silu(gate_q) * up_q).astype(jnp.bfloat16)
    output = jnp.einsum(
        "thj,hjk->thk", hidden_q, rounded[2], preferred_element_type=jnp.float32
    ).reshape(row_count, channel_count)
    mixed_rows = (stream.astype(jnp.float32) + gain_rows[4] * output).astype(jnp.bfloat16)
    gate_k = jnp.einsum("thi,hij->thj", keys_in, rounded[0], preferred_element_type=jnp.float32)
    up_k = jnp.einsum("thi,hij->thj", keys_in, rounded[1], preferred_element_type=jnp.float32)
    sigmoid_k = jax.nn.sigmoid(gate_k)
    active_k = gate_k * sigmoid_k
    hidden_k = (active_k * up_k).astype(jnp.bfloat16)
    targets = (rates_row[:, None, None] * values_in.astype(jnp.float32)).astype(jnp.bfloat16)
    back_hidden = jnp.einsum(
        "thk,hjk->thj", targets, rounded[2], preferred_element_type=jnp.float32
    )
    back_up = (back_hidden * active_k).astype(jnp.bfloat16)
    back_gate = (back_hidden * up_k * sigmoid_k * (1.0 + gate_k * (1.0 - sigmoid_k))).astype(
        jnp.bfloat16
    )
    grad_gate = jnp.einsum("thi,thj->hij", keys_in, back_gate, preferred_element_type=jnp.float32)
    grad_up = jnp.einsum("thi,thj->hij", keys_in, back_up, preferred_element_type=jnp.float32)
    grad_down = jnp.einsum("thj,thk->hjk", hidden_k, targets, preferred_element_type=jnp.float32)
    direction = orthogonalize(jnp.stack([grad_gate, grad_up, grad_down]))
    moved_state = entering + (update_flag * steps_row)[None, :, None, None] * direction
    norm_before = jnp.sqrt(jnp.sum(entering * entering, axis=2, keepdims=True) + EPSILON)
    norm_after = jnp.sqrt(jnp.sum(moved_state * moved_state, axis=2, keepdims=True) + EPSILON)
    return (mixed_rows, moved_state * (norm_before / norm_after))


def pass_on(outgoing):
    return passed_along(outgoing, "group", 1)


def body(tokens, learning_rates, channel_gains, fast_init, step_size, update_table):
    start_stream = lax.all_to_all(tokens, "tok", split_axis=1, concat_axis=0, tiled=True)
    group_count = lax.axis_size("group")
    group_index = lax.axis_index("group")
    width_all = start_stream.shape[1] * lax.axis_size("tok")
    layer_count = fast_init.shape[0]
    zero_state = jnp.zeros(fast_init.shape[1:], jnp.float32)

    def tick_work(stream, outgoing, layer_now, active, inverse):
        received = pass_on(outgoing)
        initial = lax.dynamic_index_in_dim(fast_init, layer_now, 0, keepdims=False)
        entering = jnp.where(group_index == 0, initial, received)
        gain_rows = lax.dynamic_index_in_dim(channel_gains, layer_now, 0, keepdims=False)
        rates_row = lax.dynamic_index_in_dim(learning_rates, layer_now, 0, keepdims=False)
        steps_row = lax.dynamic_index_in_dim(step_size, layer_now, 0, keepdims=False)
        table_cell = lax.dynamic_slice(
            update_table, (jnp.asarray(layer_now, jnp.int32), group_index), (1, 1)
        )
        update_flag = table_cell[0, 0].astype(jnp.float32)

        def working(operands):
            return layer_group(
                operands[0], operands[1], gain_rows, rates_row, steps_row, update_flag, inverse
            )

        def resting(operands):
            return (operands[0], operands[2])

        return lax.cond(active, working, resting, (stream, entering, outgoing))

    def one_tick(tick_index, loop_state):
        stream, outgoing = loop_state
        layer_raw = tick_index - group_index
        active = (layer_raw >= 0) & (layer_raw < layer_count)
        layer_now = jnp.clip(layer_raw, 0, layer_count - 1)
        widened = stream.astype(jnp.float32)
        totals = lax.psum(jnp.sum(widened * widened, axis=1), "tok")
        inverse = lax.rsqrt(totals / width_all + EPSILON)
        return tick_work(stream, outgoing, layer_now, active, inverse)

    final_stream, last_state = lax.fori_loop(
        0, layer_count + group_count - 1, one_tick, (start_stream, zero_state)
    )
    return lax.all_to_all(final_stream, "tok", split_axis=0, concat_axis=1, tiled=True)


MESH = pl.DeviceIdType.MESH
F32 = jnp.float32
BF16 = jnp.bfloat16
NN = (((1,), (0,)), ((), ()))
NT = (((1,), (1,)), ((), ()))
TN = (((0,), (0,)), ((), ()))


def dot(a, b, dims=NN):
    return lax.dot_general(a, b, dims, preferred_element_type=F32)


def halves(value):
    high = value.astype(BF16)
    return high, (value - high.astype(F32)).astype(BF16)


def product(a, b):
    a_high, a_low = halves(a)
    b_high, b_low = halves(b)
    left = jnp.concatenate([a_high, a_low], axis=1)
    above = jnp.concatenate([b_high, b_low], axis=1)
    below = jnp.concatenate([b_high, jnp.zeros_like(b_low)], axis=1)
    both = dot(left, jnp.concatenate([above, below], axis=0))
    return both[:, : b.shape[1]] + both[:, b.shape[1] :]


def gram(a):
    high, low = halves(a)
    left = jnp.concatenate([high, low], axis=1)
    above = jnp.concatenate([high, high], axis=1)
    below = jnp.concatenate([low, jnp.zeros_like(low)], axis=1)
    both = dot(left, jnp.concatenate([above, below], axis=0), NT)
    return both[:, : a.shape[0]] + both[:, a.shape[0] :]


def sigmoid(value):
    return 0.5 * jnp.tanh(0.5 * value) + 0.5


def newton_schulz(values):
    squares = [gram(v) for v in values]
    polynoms = [MUON_B * q + MUON_C * product(q, q) for q in squares]
    return tuple(MUON_A * v + product(p, v) for p, v in zip(polynoms, values))


def wave_kernel(
    sizes,
    steps,
    table,
    tokens,
    rates,
    gains,
    initial,
    out,
    xin,
    xout,
    weights,
    leaving,
    totals,
    squares,
    partial,
    partials,
    stack,
    grad_gu,
    grad_d,
    t_send,
    t_recv,
    s_send,
    s_recv,
    p_send,
    p_recv,
    w_send,
    w_recv,
    o_send,
    o_recv,
):
    groups, toks, layers, owned, rows, width, tile = sizes
    group_tok = rows * toks
    g = lax.axis_index("group")
    t = lax.axis_index("tok")
    last = groups - 1

    def remote(source, target, send, recv, to_g, to_t):
        return pltpu.make_async_remote_copy(
            src_ref=source,
            dst_ref=target,
            send_sem=send,
            recv_sem=recv,
            device_id=(to_g, to_t),
            device_id_type=MESH,
        )

    def arrived(target, recv):
        pltpu.make_async_copy(target, target, recv).wait()

    def lane(index, size):
        return pl.ds(pl.multiple_of(index * size, size), size)

    barrier = pltpu.get_barrier_semaphore()

    def greet(to_g, to_t):
        pl.semaphore_signal(barrier, inc=1, device_id=(to_g, to_t), device_id_type=MESH)

    for step in range(1, toks):
        greet(g, lax.rem(t + step, toks))

    greet(lax.rem(g + 1, groups), t)
    greet(lax.rem(g + last, groups), t)
    pl.semaphore_wait(barrier, toks + 1)

    def peer(step):
        return lax.rem(t + step, toks)

    def hand_out(j):
        for step in [2, 3, 1, 0] if toks == 4 else range(toks):
            to_t = peer(step)
            source = tokens.at[:, lane(to_t * owned + j, width)]
            target = xin.at[0, j, lane(t, rows)]
            if step == 0:
                pltpu.make_async_copy(source, target, t_recv.at[j, t]).start()
            else:
                remote(source, target, t_send.at[j, step], t_recv.at[j, t], g, to_t).start()

    hand_out(0)
    ones_rows = jnp.ones((16, width), BF16)

    def sums_of(values):
        wide = values.astype(F32)
        return dot(ones_rows, (wide * wide).astype(BF16), NT)[0:1]

    totals[...] = jnp.zeros_like(totals)

    @pl.loop(0, owned * toks)
    def _(h):
        totals[...] += sums_of(tokens[:, lane(h, width)])

    squares[t] = totals[...]
    for step in range(1, toks):
        remote(totals, squares.at[t], s_send.at[step], s_recv.at[t], g, peer(step)).start()

    @pl.loop(1, owned)
    def _(j):
        hand_out(j)

    @pl.when(g == 0)
    def _():
        for l in range(layers):
            @pl.loop(0, owned)
            def _(j):
                for which in range(3):
                    weights[l, j, :, which * width : (which + 1) * width] = initial[
                        l, which, j
                    ].astype(BF16)

    pick_row = lax.broadcasted_iota(jnp.int32, (16, 2 * width), 0)
    pick_lane = lax.broadcasted_iota(jnp.int32, (16, 2 * width), 1)
    spread = jnp.where(pick_row // 2 == pick_lane // width, 1.0, 0.0).astype(BF16)

    def scale_rows(l, at, sums):
        size = sums.shape[1]
        inverse = lax.rsqrt(sums / (owned * toks * width) + EPSILON)
        rate = rates[l : l + 1, at]
        inverse_high = inverse.astype(BF16).astype(F32)
        rate_high = rate.astype(BF16).astype(F32)
        at_row = lax.broadcasted_iota(jnp.int32, (16, size), 0)
        fill = jnp.where(at_row == 0, inverse_high, 0.0)
        fill = jnp.where(at_row == 1, inverse - inverse_high, fill)
        fill = jnp.where(at_row == 2, rate_high, fill)
        stack[:, at] = jnp.where(at_row == 3, rate - rate_high, fill).astype(BF16)

    def gains_of(l, j):
        rows_of = gains[l, :, lane(j, width)]
        norm = rows_of[0:1]
        return norm * rows_of[1:2], norm * rows_of[2:3], norm * rows_of[3:4], rows_of[4:5]

    def query(l, j):
        query_gain, _, _, out_gain = gains_of(l, j)
        size = min(tile, group_tok)

        @pl.loop(0, group_tok // size)
        def _(i):
            here = lane(i, size)
            stream = xin[l, j, here, :].astype(F32)
            normed = stream * dot(stack[:, here], spread[:, :width], TN)
            queries = (normed * query_gain).astype(BF16)
            both = dot(queries, weights[l, j, :, : 2 * width])
            gate = both[:, :width]
            hidden = (gate * sigmoid(gate) * both[:, width:]).astype(BF16)
            mixed = (stream + out_gain * dot(hidden, weights[l, j, :, 2 * width :])).astype(BF16)
            if l < layers - 1:
                xin[l + 1, j, here, :] = mixed
                partial[l, :, here] += sums_of(mixed)
            else:
                xout[j, here, :] = mixed

        if l == layers - 1:
            for step in [2, 3, 1, 0] if toks == 4 else range(toks):
                to_t = peer(step)
                source = xout.at[j, lane(to_t, rows)]
                target = out.at[:, lane(t * owned + j, width)]
                if step == 0:
                    pltpu.make_async_copy(source, target, o_recv).start()
                else:
                    remote(source, target, o_send.at[j, step], o_recv, g, to_t).start()

    def learn(l, j):
        _, key_gain, value_gain, _ = gains_of(l, j)
        size = min(tile, group_tok)
        grad_gu[...] = jnp.zeros_like(grad_gu)
        grad_d[...] = jnp.zeros_like(grad_d)

        @pl.loop(0, group_tok // size)
        def _(i):
            here = lane(i, size)
            scale = dot(stack[:, here], spread, TN)
            normed = xin[l, j, here, :].astype(F32) * scale[:, :width]
            keys = (normed * key_gain).astype(BF16)
            targets = (normed * value_gain * scale[:, width:]).astype(BF16)
            both = dot(keys, weights[l, j, :, : 2 * width])
            back = dot(targets, weights[l, j, :, 2 * width :], NT)
            gate = both[:, :width]
            up = both[:, width:]
            sig = sigmoid(gate)
            act = gate * sig
            hidden = (act * up).astype(BF16)
            back_up = (back * act).astype(BF16)
            back_gate = (back * up * (sig + act * (1.0 - sig))).astype(BF16)
            backs = jnp.concatenate([back_gate, back_up], axis=1)
            grad_gu[...] += dot(keys, backs, TN)
            grad_d[...] += dot(hidden, targets, TN)

    def chain(l, j):
        @pl.when(g > 0)
        def _():
            arrived(weights.at[l, j], w_recv.at[l, j])

        chain_go(l, j)

    def chain_go(l, j):
        @pl.when(g < last)
        def _():
            learn(l, j)
            grads = (grad_gu[:, :width], grad_gu[:, width:], grad_d[...])
            moves = tuple(
                v * lax.rsqrt(jnp.sum(v * v, axis=(0, 1), keepdims=True) + EPSILON) for v in grads
            )
            for _ in range(NS_STEPS):
                moves = newton_schulz(moves)
            step = steps[l, j] * table[l, g].astype(F32)
            for which in range(3):
                at = slice(which * width, (which + 1) * width)
                entering = weights[l, j, :, at].astype(F32)
                moved = entering + step * moves[which]
                before = jnp.sum(entering * entering, axis=0, keepdims=True) + EPSILON
                after = jnp.sum(moved * moved, axis=0, keepdims=True) + EPSILON
                leaving[l, j, :, at] = (moved * (jnp.sqrt(before) * lax.rsqrt(after))).astype(BF16)
            remote(
                leaving.at[l, j], weights.at[l, j], w_send.at[l, j], w_recv.at[l, j], g + 1, t
            ).start()

    def await_tokens(j):
        for k in range(toks):
            arrived(xin.at[0, j, pl.ds(k * rows, rows)], t_recv.at[j, k])

    for step in range(1, toks):
        arrived(squares.at[peer(step)], s_recv.at[peer(step)])
    for k in range(toks):
        scale_rows(0, slice(k * rows, (k + 1) * rows), squares[k])

    for l in range(layers):
        if l > 0:
            arrived_sums = partial[l - 1]
            for step in range(1, toks):
                arrived(partials.at[l - 1, peer(step)], p_recv.at[l - 1, peer(step)])
                arrived_sums += partials[l - 1, peer(step)]
            scale_rows(l, slice(0, group_tok), arrived_sums)
        if l < layers - 1:
            partial[l] = jnp.zeros((1, group_tok), F32)

            @pl.loop(0, owned - 1)
            def _(j):
                if l == 0:
                    await_tokens(j)
                chain(l, j)
                query(l, j)

            if l == 0:
                await_tokens(owned - 1)

            @pl.when(g > 0)
            def _():
                arrived(weights.at[l, owned - 1], w_recv.at[l, owned - 1])

            query(l, owned - 1)
            for step in range(1, toks):
                remote(
                    partial.at[l],
                    partials.at[l, t],
                    p_send.at[l, step],
                    p_recv.at[l, t],
                    g,
                    peer(step),
                ).start()
            chain_go(l, owned - 1)
        else:
            @pl.loop(0, owned)
            def _(j):
                chain(l, j)

                @pl.when(g == last)
                def _():
                    query(l, j)

            @pl.when(g < last)
            def _():
                @pl.loop(0, owned)
                def _(j):
                    query(l, j)

    arrived(out, o_recv)

    @pl.loop(0, owned)
    def _(j):
        for step in range(1, toks):
            source = tokens.at[:, lane(peer(step) * owned + j, width)]
            pltpu.make_async_copy(source, source, t_send.at[j, step]).wait()
            block = xout.at[j, lane(peer(step), rows)]
            pltpu.make_async_copy(block, block, o_send.at[j, step]).wait()

        @pl.when(g < last)
        def _():
            for l in range(layers):
                arrived(leaving.at[l, j], w_send.at[l, j])

    for step in range(1, toks):
        arrived(totals, s_send.at[step])
        for l in range(layers - 1):
            arrived(partial.at[l], p_send.at[l, step])


def wave_body(tokens, learning_rates, channel_gains, fast_init, step_size, update_table):
    groups, toks = lax.axis_size("group"), lax.axis_size("tok")
    layers, _, owned, width, _ = fast_init.shape
    rows, channels = tokens.shape
    group_tok = rows * toks
    sizes = (groups, toks, layers, owned, rows, width, TILE)
    vmem = pl.BlockSpec(memory_space=pltpu.VMEM)
    smem = pl.BlockSpec(memory_space=pltpu.SMEM)
    anywhere = pl.BlockSpec(memory_space=pl.ANY)
    dma = pltpu.SemaphoreType.DMA
    return pl.pallas_call(
        functools.partial(wave_kernel, sizes),
        out_shape=jax.ShapeDtypeStruct((rows, channels), BF16),
        in_specs=[smem, smem, vmem, vmem, vmem, vmem],
        out_specs=anywhere,
        scratch_shapes=[
            pltpu.VMEM((layers, owned, group_tok, width), BF16),
            pltpu.VMEM((owned, group_tok, width), BF16),
            pltpu.VMEM((layers, owned, width, 3 * width), BF16),
            pltpu.VMEM((layers, owned, width, 3 * width), BF16),
            pltpu.VMEM((1, rows), F32),
            pltpu.VMEM((toks, 1, rows), F32),
            pltpu.VMEM((layers - 1, 1, group_tok), F32),
            pltpu.VMEM((layers - 1, toks, 1, group_tok), F32),
            pltpu.VMEM((16, group_tok), BF16),
            pltpu.VMEM((width, 2 * width), F32),
            pltpu.VMEM((width, width), F32),
            dma((owned, toks)),
            dma((owned, toks)),
            dma((toks,)),
            dma((toks,)),
            dma((layers - 1, toks)),
            dma((layers - 1, toks)),
            dma((layers, owned)),
            dma((layers, owned)),
            dma((owned, toks)),
            dma,
        ],
        compiler_params=pltpu.CompilerParams(
            collective_id=0, has_side_effects=True, vmem_limit_bytes=48 * 1024 * 1024
        ),
    )(step_size, update_table, tokens, learning_rates, channel_gains, fast_init)


TILE = 1024


def plan(mesh, tokens, fast_init):
    groups, toks = mesh.shape["group"], mesh.shape["tok"]
    layers, _, heads, width, _ = fast_init.shape
    rows = tokens.shape[0] // (groups * toks)
    fits = groups > 1 and toks > 1 and layers > 1 and heads % toks == 0
    fits = fits and rows * toks % TILE == 0 and rows % 128 == 0 and width % 128 == 0
    return wave_body if fits and tokens.shape[0] * tokens.shape[1] <= 64 * 1024 * 1024 else body


def solution(mesh):
    in_specs = (
        P(("group", "tok"), None),
        P(None, "group"),
        P(None, None, "tok"),
        P(None, None, "tok", None, None),
        P(None, "tok"),
        P(),
    )
    out_specs = P(("group", "tok"), None)
    def run(*args):
        chosen = plan(mesh, args[0], args[3])
        return jax.shard_map(
            chosen, mesh=mesh, in_specs=in_specs, out_specs=out_specs, check_vma=False
        )(*args)

    return run
```

time: 173 us -> 146 us (0.84)
  the two profiles are of different devices: /device:TPU:29 before, /device:TPU:25 now
where the time goes in v1:
time: 146 us
  Pallas kernels  138 us (95%)
  local copies, waits for them, and re-layouts  7.12 us (5%)
    pallas_call x1, Pallas kernels, wave_body(): pl.pallas_call(functools.partial(wave_kernel, sizes), out_shape=jax.Shape...  138 us
    unnamed x12, local copies, waits for them, and re-layouts  7.12 us

profile of v1, /device:TPU:25, one launch (start us, length us, event | category | flops | bytes accessed | tf_op | source)
XLA Modules:
  0.0 145.6 jit_solution(5839076606828800263)
XLA Ops:
  0.0 0.7 copy.7.gains
  0.7 0.0 copy-start
  0.7 1.6 %copy-done = bf16[512,2048]{1,0:T(8,128)(2,1)S(1)} copy-done((bf16[512,2048]{1,0:T(8,128)(2,1)S(1)}, bf16[512,2048]{1,0:T(8,128)(2,1)}, u32[]{:S(2)}) %copy-start) | copy-done | bytes 2097176
  2.3 0.0 copy-start.1
  2.3 1.4 copy-done.1
  3.7 0.0 copy-start.2
  3.7 0.7 copy-done.2
  4.5 0.0 copy-start.3
  4.5 0.7 copy-done.3
  5.1 0.0 copy-start.4
  5.1 0.7 copy-done.4
  5.8 138.4 %shard_map.64 = bf16[512,2048]{1,0:T(8,128)(2,1)S(1)} custom-call(f32[2,4]{1,0:T(2,128)S(1)} %copy-done.3, s32[2,8]{1,0:T(2,128)S(1)} %copy-done.4, bf16[512,2048]{1,0:T(8,128)(2,1)S(1)} %copy-done, f32[2,2048]{1,0:T(2,128)S(1)} %copy-done.2, f32[2,5,512]{2,1,0:T(8,128)S(1)} %copy.7.gains, f32[2,3,4,128,128]{4,3,2,1,0:T(8,128)S(1)} %copy-done.1), custom_call_target="tpu_custom_call" | custom-call | tf_op jit(solution)/shard_map/pallas_call | solution.py:479
  144.3 1.3 copy.9
Async XLA Ops:
  0.7 1.6 %copy-start = (bf16[512,2048]{1,0:T(8,128)(2,1)S(1)}, bf16[512,2048]{1,0:T(8,128)(2,1)}, u32[]{:S(2)}) copy-start(bf16[512,2048]{1,0:T(8,128)(2,1)} %tokens.1) | copy-start | bytes 6291460
  2.3 1.4 copy-start.1
  3.7 0.7 copy-start.2
  4.5 0.7 copy-start.3
  5.1 0.7 copy-start.4

commit v2 on v1

--- a/solution.py
+++ b/solution.py
@@ -137,49 +137,31 @@
     return lax.dot_general(a, b, dims, preferred_element_type=F32)
 
 
-def halves(value):
-    high = value.astype(BF16)
-    return high, (value - high.astype(F32)).astype(BF16)
-
-
-def product(a, b):
-    a_high, a_low = halves(a)
-    b_high, b_low = halves(b)
-    left = jnp.concatenate([a_high, a_low], axis=1)
-    above = jnp.concatenate([b_high, b_low], axis=1)
-    below = jnp.concatenate([b_high, jnp.zeros_like(b_low)], axis=1)
-    both = dot(left, jnp.concatenate([above, below], axis=0))
-    return both[:, : b.shape[1]] + both[:, b.shape[1] :]
-
-
-def gram(a):
-    high, low = halves(a)
-    left = jnp.concatenate([high, low], axis=1)
-    above = jnp.concatenate([high, high], axis=1)
-    below = jnp.concatenate([low, jnp.zeros_like(low)], axis=1)
-    both = dot(left, jnp.concatenate([above, below], axis=0), NT)
-    return both[:, : a.shape[0]] + both[:, a.shape[0] :]
-
-
 def sigmoid(value):
     return 0.5 * jnp.tanh(0.5 * value) + 0.5
 
 
 def newton_schulz(values):
-    squares = [gram(v) for v in values]
-    polynoms = [MUON_B * q + MUON_C * product(q, q) for q in squares]
-    return tuple(MUON_A * v + product(p, v) for p, v in zip(polynoms, values))
+    rounded = [v.astype(BF16) for v in values]
+    squares = [dot(v, v, NT) for v in rounded]
+    narrow = [q.astype(BF16) for q in squares]
+    polynoms = [(MUON_B * q + MUON_C * dot(n, n)).astype(BF16) for q, n in zip(squares, narrow)]
+    return tuple(MUON_A * v + dot(p, r) for p, v, r in zip(polynoms, values, rounded))
 
 
 def wave_kernel(
     sizes,
     steps,
     table,
+    tokens_in,
+    rates_in,
+    gains_in,
+    initial_in,
+    out,
     tokens,
     rates,
     gains,
     initial,
-    out,
     xin,
     xout,
     weights,
@@ -201,6 +183,7 @@
     w_recv,
     o_send,
     o_recv,
+    i_recv,
 ):
     groups, toks, layers, owned, rows, width, tile = sizes
     group_tok = rows * toks
@@ -224,31 +207,44 @@
     def lane(index, size):
         return pl.ds(pl.multiple_of(index * size, size), size)
 
+    loads = [
+        pltpu.make_async_copy(source, target, i_recv.at[i])
+        for i, (source, target) in enumerate(
+            [(tokens_in, tokens), (rates_in, rates), (gains_in, gains), (initial_in, initial)]
+        )
+    ]
+    for load in loads[:3]:
+        load.start()
+
+    @pl.when(g == 0)
+    def _():
+        loads[3].start()
+
     barrier = pltpu.get_barrier_semaphore()
 
     def greet(to_g, to_t):
         pl.semaphore_signal(barrier, inc=1, device_id=(to_g, to_t), device_id_type=MESH)
 
-    for step in range(1, toks):
-        greet(g, lax.rem(t + step, toks))
+    chip, core = t // 2, lax.rem(t, 2)
+    peers = [
+        lax.rem(chip + far, toks // 2) * 2 + side for far in range(1, toks // 2) for side in range(2)
+    ] + [t + 1 - 2 * core]
+    for to_t in peers:
+        greet(g, to_t)
 
     greet(lax.rem(g + 1, groups), t)
     greet(lax.rem(g + last, groups), t)
     pl.semaphore_wait(barrier, toks + 1)
 
-    def peer(step):
-        return lax.rem(t + step, toks)
-
     def hand_out(j):
-        for step in [2, 3, 1, 0] if toks == 4 else range(toks):
-            to_t = peer(step)
+        target = xin.at[0, j, lane(t, rows)]
+        for i, to_t in enumerate(peers):
             source = tokens.at[:, lane(to_t * owned + j, width)]
-            target = xin.at[0, j, lane(t, rows)]
-            if step == 0:
-                pltpu.make_async_copy(source, target, t_recv.at[j, t]).start()
-            else:
-                remote(source, target, t_send.at[j, step], t_recv.at[j, t], g, to_t).start()
-
+            remote(source, target, t_send.at[j, i], t_recv.at[j, t], g, to_t).start()
+        source = tokens.at[:, lane(t * owned + j, width)]
+        pltpu.make_async_copy(source, target, t_recv.at[j, t]).start()
+
+    loads[0].wait()
     hand_out(0)
     ones_rows = jnp.ones((16, width), BF16)
 
@@ -263,15 +259,19 @@
         totals[...] += sums_of(tokens[:, lane(h, width)])
 
     squares[t] = totals[...]
-    for step in range(1, toks):
-        remote(totals, squares.at[t], s_send.at[step], s_recv.at[t], g, peer(step)).start()
+    for i, to_t in enumerate(peers):
+        remote(totals, squares.at[t], s_send.at[i], s_recv.at[t], g, to_t).start()
 
     @pl.loop(1, owned)
     def _(j):
         hand_out(j)
 
+    loads[1].wait()
+    loads[2].wait()
+
     @pl.when(g == 0)
     def _():
+        loads[3].wait()
         for l in range(layers):
             @pl.loop(0, owned)
             def _(j):
@@ -322,23 +322,17 @@
                 xout[j, here, :] = mixed
 
         if l == layers - 1:
-            for step in [2, 3, 1, 0] if toks == 4 else range(toks):
-                to_t = peer(step)
+            target = out.at[:, lane(t * owned + j, width)]
+            for i, to_t in enumerate(peers):
                 source = xout.at[j, lane(to_t, rows)]
-                target = out.at[:, lane(t * owned + j, width)]
-                if step == 0:
-                    pltpu.make_async_copy(source, target, o_recv).start()
-                else:
-                    remote(source, target, o_send.at[j, step], o_recv, g, to_t).start()
+                remote(source, target, o_send.at[j, i], o_recv, g, to_t).start()
+            pltpu.make_async_copy(xout.at[j, lane(t, rows)], target, o_recv).start()
 
     def learn(l, j):
         _, key_gain, value_gain, _ = gains_of(l, j)
         size = min(tile, group_tok)
-        grad_gu[...] = jnp.zeros_like(grad_gu)
-        grad_d[...] = jnp.zeros_like(grad_d)
-
-        @pl.loop(0, group_tok // size)
-        def _(i):
+
+        def found(i):
             here = lane(i, size)
             scale = dot(stack[:, here], spread, TN)
             normed = xin[l, j, here, :].astype(F32) * scale[:, :width]
@@ -354,8 +348,20 @@
             back_up = (back * act).astype(BF16)
             back_gate = (back * up * (sig + act * (1.0 - sig))).astype(BF16)
             backs = jnp.concatenate([back_gate, back_up], axis=1)
-            grad_gu[...] += dot(keys, backs, TN)
-            grad_d[...] += dot(hidden, targets, TN)
+            return dot(keys, backs, TN), dot(hidden, targets, TN)
+
+        if size == group_tok:
+            return found(0)
+        grad_gu[...] = jnp.zeros_like(grad_gu)
+        grad_d[...] = jnp.zeros_like(grad_d)
+
+        @pl.loop(0, group_tok // size)
+        def _(i):
+            more_gu, more_d = found(i)
+            grad_gu[...] += more_gu
+            grad_d[...] += more_d
+
+        return grad_gu[...], grad_d[...]
 
     def chain(l, j):
         @pl.when(g > 0)
@@ -367,8 +373,8 @@
     def chain_go(l, j):
         @pl.when(g < last)
         def _():
-            learn(l, j)
-            grads = (grad_gu[:, :width], grad_gu[:, width:], grad_d[...])
+            both, below = learn(l, j)
+            grads = (both[:, :width], both[:, width:], below)
             moves = tuple(
                 v * lax.rsqrt(jnp.sum(v * v, axis=(0, 1), keepdims=True) + EPSILON) for v in grads
             )
@@ -390,17 +396,17 @@
         for k in range(toks):
             arrived(xin.at[0, j, pl.ds(k * rows, rows)], t_recv.at[j, k])
 
-    for step in range(1, toks):
-        arrived(squares.at[peer(step)], s_recv.at[peer(step)])
+    for to_t in peers:
+        arrived(squares.at[to_t], s_recv.at[to_t])
     for k in range(toks):
         scale_rows(0, slice(k * rows, (k + 1) * rows), squares[k])
 
     for l in range(layers):
         if l > 0:
             arrived_sums = partial[l - 1]
-            for step in range(1, toks):
-                arrived(partials.at[l - 1, peer(step)], p_recv.at[l - 1, peer(step)])
-                arrived_sums += partials[l - 1, peer(step)]
+            for to_t in peers:
+                arrived(partials.at[l - 1, to_t], p_recv.at[l - 1, to_t])
+                arrived_sums += partials[l - 1, to_t]
             scale_rows(l, slice(0, group_tok), arrived_sums)
         if l < layers - 1:
             partial[l] = jnp.zeros((1, group_tok), F32)
@@ -420,14 +426,9 @@
                 arrived(weights.at[l, owned - 1], w_recv.at[l, owned - 1])
 
             query(l, owned - 1)
-            for step in range(1, toks):
+            for i, to_t in enumerate(peers):
                 remote(
-                    partial.at[l],
-                    partials.at[l, t],
-                    p_send.at[l, step],
-                    p_recv.at[l, t],
-                    g,
-                    peer(step),
+                    partial.at[l], partials.at[l, t], p_send.at[l, i], p_recv.at[l, t], g, to_t
                 ).start()
             chain_go(l, owned - 1)
         else:
@@ -449,21 +450,19 @@
 
     @pl.loop(0, owned)
     def _(j):
-        for step in range(1, toks):
-            source = tokens.at[:, lane(peer(step) * owned + j, width)]
-            pltpu.make_async_copy(source, source, t_send.at[j, step]).wait()
-            block = xout.at[j, lane(peer(step), rows)]
-            pltpu.make_async_copy(block, block, o_send.at[j, step]).wait()
+        for i, to_t in enumerate(peers):
+            arrived(tokens.at[:, lane(to_t * owned + j, width)], t_send.at[j, i])
+            arrived(xout.at[j, lane(to_t, rows)], o_send.at[j, i])
 
         @pl.when(g < last)
         def _():
             for l in range(layers):
                 arrived(leaving.at[l, j], w_send.at[l, j])
 
-    for step in range(1, toks):
-        arrived(totals, s_send.at[step])
+    for i in range(toks - 1):
+        arrived(totals, s_send.at[i])
         for l in range(layers - 1):
-            arrived(partial.at[l], p_send.at[l, step])
+            arrived(partial.at[l], p_send.at[l, i])
 
 
 def wave_body(tokens, learning_rates, channel_gains, fast_init, step_size, update_table):
@@ -472,16 +471,19 @@
     rows, channels = tokens.shape
     group_tok = rows * toks
     sizes = (groups, toks, layers, owned, rows, width, TILE)
-    vmem = pl.BlockSpec(memory_space=pltpu.VMEM)
     smem = pl.BlockSpec(memory_space=pltpu.SMEM)
     anywhere = pl.BlockSpec(memory_space=pl.ANY)
     dma = pltpu.SemaphoreType.DMA
     return pl.pallas_call(
         functools.partial(wave_kernel, sizes),
         out_shape=jax.ShapeDtypeStruct((rows, channels), BF16),
-        in_specs=[smem, smem, vmem, vmem, vmem, vmem],
+        in_specs=[smem, smem, anywhere, anywhere, anywhere, anywhere],
         out_specs=anywhere,
         scratch_shapes=[
+            pltpu.VMEM(tokens.shape, BF16),
+            pltpu.VMEM(learning_rates.shape, F32),
+            pltpu.VMEM(channel_gains.shape, F32),
+            pltpu.VMEM(fast_init.shape, F32),
             pltpu.VMEM((layers, owned, group_tok, width), BF16),
             pltpu.VMEM((owned, group_tok, width), BF16),
             pltpu.VMEM((layers, owned, width, 3 * width), BF16),
@@ -503,6 +505,7 @@
             dma((layers, owned)),
             dma((owned, toks)),
             dma,
+            dma((4,)),
         ],
         compiler_params=pltpu.CompilerParams(
             collective_id=0, has_side_effects=True, vmem_limit_bytes=48 * 1024 * 1024
@@ -510,14 +513,14 @@
     )(step_size, update_table, tokens, learning_rates, channel_gains, fast_init)
 
 
-TILE = 1024
+TILE = 2048
 
 
 def plan(mesh, tokens, fast_init):
     groups, toks = mesh.shape["group"], mesh.shape["tok"]
     layers, _, heads, width, _ = fast_init.shape
     rows = tokens.shape[0] // (groups * toks)
-    fits = groups > 1 and toks > 1 and layers > 1 and heads % toks == 0
+    fits = groups > 1 and toks > 2 and toks % 2 == 0 and layers > 1 and heads % toks == 0
     fits = fits and rows * toks % TILE == 0 and rows % 128 == 0 and width % 128 == 0
     return wave_body if fits and tokens.shape[0] * tokens.shape[1] <= 64 * 1024 * 1024 else body
 

time: 146 us -> 131 us (0.90)
  Pallas kernels: 138 us -> 123 us
    pallas_call x1, Pallas kernels: 138 us -> 123 us  [wave_body(): pl.pallas_call(functools.partial(wave_kernel, sizes), out_shape=jax.Shape...]
where the time goes in v2:
time: 131 us
  Pallas kernels  123 us (94%)
  local copies, waits for them, and re-layouts  7.12 us (5%)
    pallas_call x1, Pallas kernels, wave_body(): pl.pallas_call(functools.partial(wave_kernel, sizes), out_shape=jax.Shape...  123 us
    unnamed x12, local copies, waits for them, and re-layouts  7.12 us

profile of v2, /device:TPU:25, one launch (start us, length us, event | category | flops | bytes accessed | tf_op | source)
XLA Modules:
  0.0 130.6 jit_solution(1734097237707743371)
XLA Ops:
  0.0 0.7 copy.7.gains_in
  0.7 0.0 copy-start
  0.7 1.6 %copy-done = bf16[512,2048]{1,0:T(8,128)(2,1)S(1)} copy-done((bf16[512,2048]{1,0:T(8,128)(2,1)S(1)}, bf16[512,2048]{1,0:T(8,128)(2,1)}, u32[]{:S(2)}) %copy-start) | copy-done | bytes 2097176
  2.3 0.0 copy-start.1
  2.3 1.4 %copy-done.1 = f32[2,3,4,128,128]{4,3,2,1,0:T(8,128)S(1)} copy-done((f32[2,3,4,128,128]{4,3,2,1,0:T(8,128)S(1)}, f32[2,3,4,128,128]{4,3,2,1,0:T(8,128)}, u32[]{:S(2)}) %copy-start.1) | copy-done | bytes 1572888
  3.7 0.0 copy-start.2
  3.7 0.7 copy-done.2
  4.5 0.0 copy-start.3
  4.5 0.7 copy-done.3
  5.1 0.0 copy-start.4
  5.1 0.7 copy-done.4
  5.8 123.5 %shard_map.64 = bf16[512,2048]{1,0:T(8,128)(2,1)S(1)} custom-call(f32[2,4]{1,0:T(2,128)S(1)} %copy-done.3, s32[2,8]{1,0:T(2,128)S(1)} %copy-done.4, bf16[512,2048]{1,0:T(8,128)(2,1)S(1)} %copy-done, f32[2,2048]{1,0:T(2,128)S(1)} %copy-done.2, f32[2,5,512]{2,1,0:T(8,128)S(1)} %copy.7.gains_in, f32[2,3,4,128,128]{4,3,2,1,0:T(8,128)S(1)} %copy-done.1), custom_call_target="tpu_custom_call" | custom-call | tf_op jit(solution)/shard_map/pallas_call | solution.py:477
  129.3 1.3 %copy.9 = bf16[512,2048]{1,0:T(8,128)(2,1)} copy(bf16[512,2048]{1,0:T(8,128)(2,1)S(1)} %shard_map.64) | data formatting | bytes 4194304
Async XLA Ops:
  0.7 1.6 %copy-start = (bf16[512,2048]{1,0:T(8,128)(2,1)S(1)}, bf16[512,2048]{1,0:T(8,128)(2,1)}, u32[]{:S(2)}) copy-start(bf16[512,2048]{1,0:T(8,128)(2,1)} %tokens_in.1) | copy-start | bytes 6291460
  2.3 1.4 %copy-start.1 = (f32[2,3,4,128,128]{4,3,2,1,0:T(8,128)S(1)}, f32[2,3,4,128,128]{4,3,2,1,0:T(8,128)}, u32[]{:S(2)}) copy-start(f32[2,3,4,128,128]{4,3,2,1,0:T(8,128)} %initial_in.1) | copy-start | bytes 4718596
  3.7 0.7 copy-start.2
  4.5 0.7 copy-start.3
  5.1 0.7 copy-start.4

commit v3 on v2

--- a/solution.py
+++ b/solution.py
@@ -137,27 +137,47 @@
     return lax.dot_general(a, b, dims, preferred_element_type=F32)
 
 
+def halves(value):
+    high = value.astype(BF16)
+    return high, (value - high.astype(F32)).astype(BF16)
+
+
+def product(a, b):
+    a_high, a_low = halves(a)
+    b_high, b_low = halves(b)
+    left = jnp.concatenate([a_high, a_low], axis=1)
+    above = jnp.concatenate([b_high, b_low], axis=1)
+    below = jnp.concatenate([b_high, jnp.zeros_like(b_low)], axis=1)
+    both = dot(left, jnp.concatenate([above, below], axis=0))
+    return both[:, : b.shape[1]] + both[:, b.shape[1] :]
+
+
 def sigmoid(value):
     return 0.5 * jnp.tanh(0.5 * value) + 0.5
 
 
-def newton_schulz(values):
+def coarse(a, b):
+    return dot(a.astype(BF16), b.astype(BF16))
+
+
+def newton_schulz(values, times):
     rounded = [v.astype(BF16) for v in values]
     squares = [dot(v, v, NT) for v in rounded]
-    narrow = [q.astype(BF16) for q in squares]
-    polynoms = [(MUON_B * q + MUON_C * dot(n, n)).astype(BF16) for q, n in zip(squares, narrow)]
-    return tuple(MUON_A * v + dot(p, r) for p, v, r in zip(polynoms, values, rounded))
+    polynoms = [MUON_B * q + MUON_C * times(q, q) for q in squares]
+    return tuple(MUON_A * v + times(p, v) for p, v in zip(polynoms, values))
 
 
 def wave_kernel(
     sizes,
-    steps,
-    table,
+    steps_in,
+    table_in,
     tokens_in,
     rates_in,
     gains_in,
     initial_in,
     out,
+    steps,
+    table,
     tokens,
     rates,
     gains,
@@ -184,6 +204,9 @@
     o_send,
     o_recv,
     i_recv,
+    passing,
+    q_send,
+    q_recv,
 ):
     groups, toks, layers, owned, rows, width, tile = sizes
     group_tok = rows * toks
@@ -210,15 +233,22 @@
     loads = [
         pltpu.make_async_copy(source, target, i_recv.at[i])
         for i, (source, target) in enumerate(
-            [(tokens_in, tokens), (rates_in, rates), (gains_in, gains), (initial_in, initial)]
+            [
+                (tokens_in, tokens),
+                (rates_in, rates),
+                (gains_in, gains),
+                (steps_in, steps),
+                (table_in, table),
+                (initial_in, initial),
+            ]
         )
     ]
-    for load in loads[:3]:
+    for load in loads[:5]:
         load.start()
 
     @pl.when(g == 0)
     def _():
-        loads[3].start()
+        loads[5].start()
 
     barrier = pltpu.get_barrier_semaphore()
 
@@ -234,7 +264,16 @@
 
     greet(lax.rem(g + 1, groups), t)
     greet(lax.rem(g + last, groups), t)
-    pl.semaphore_wait(barrier, toks + 1)
+    far = toks - 2
+    for away in (2, groups - 2):
+        near_g = lax.rem(g + away, groups)
+        greet(near_g, t)
+        for to_t in peers[:far]:
+            greet(near_g, to_t)
+    pl.semaphore_wait(barrier, toks + 3 + 2 * far)
+    relays = (groups - 3, 1)
+    share = rows // 64 * 16
+    kept = rows - 2 * share
 
     def hand_out(j):
         target = xin.at[0, j, lane(t, rows)]
@@ -266,12 +305,12 @@
     def _(j):
         hand_out(j)
 
-    loads[1].wait()
-    loads[2].wait()
+    for load in loads[1:5]:
+        load.wait()
 
     @pl.when(g == 0)
     def _():
-        loads[3].wait()
+        loads[5].wait()
         for l in range(layers):
             @pl.loop(0, owned)
             def _(j):
@@ -297,7 +336,7 @@
         stack[:, at] = jnp.where(at_row == 3, rate - rate_high, fill).astype(BF16)
 
     def gains_of(l, j):
-        rows_of = gains[l, :, lane(j, width)]
+        rows_of = gains[:, l, lane(j, width)]
         norm = rows_of[0:1]
         return norm * rows_of[1:2], norm * rows_of[2:3], norm * rows_of[3:4], rows_of[4:5]
 
@@ -323,9 +362,27 @@
 
         if l == layers - 1:
             target = out.at[:, lane(t * owned + j, width)]
-            for i, to_t in enumerate(peers):
-                source = xout.at[j, lane(to_t, rows)]
-                remote(source, target, o_send.at[j, i], o_recv, g, to_t).start()
+
+            @pl.when(g < last)
+            def _():
+                for i, to_t in enumerate(peers):
+                    source = xout.at[j, lane(to_t, rows)]
+                    remote(source, target, o_send.at[j, i], o_recv, g, to_t).start()
+
+            @pl.when(g == last)
+            def _():
+                for i, to_t in enumerate(peers[:far]):
+                    for r, relay in enumerate(relays):
+                        source = xout.at[j, pl.ds(to_t * rows + kept + r * share, share)]
+                        remote(
+                            source, passing.at[j, i], q_send.at[r, j, i], q_recv.at[j, i], relay, t
+                        ).start()
+                for i, to_t in enumerate(peers[:far]):
+                    source = xout.at[j, pl.ds(to_t * rows, kept)]
+                    remote(source, target.at[:kept], o_send.at[j, i], o_recv, g, to_t).start()
+                source = xout.at[j, lane(peers[far], rows)]
+                remote(source, target, o_send.at[j, far], o_recv, g, peers[far]).start()
+
             pltpu.make_async_copy(xout.at[j, lane(t, rows)], target, o_recv).start()
 
     def learn(l, j):
@@ -378,8 +435,8 @@
             moves = tuple(
                 v * lax.rsqrt(jnp.sum(v * v, axis=(0, 1), keepdims=True) + EPSILON) for v in grads
             )
-            for _ in range(NS_STEPS):
-                moves = newton_schulz(moves)
+            for repeat in range(NS_STEPS):
+                moves = newton_schulz(moves, coarse if repeat < 2 else product)
             step = steps[l, j] * table[l, g].astype(F32)
             for which in range(3):
                 at = slice(which * width, (which + 1) * width)
@@ -446,13 +503,42 @@
                 def _(j):
                     query(l, j)
 
+    for r, relay in enumerate(relays):
+
+        @pl.when(g == relay)
+        def _():
+            @pl.loop(0, owned)
+            def _(j):
+                for i, to_t in enumerate(peers[:far]):
+                    arrived(passing.at[j, i], q_recv.at[j, i])
+                    target = out.at[pl.ds(kept + r * share, share), lane(t * owned + j, width)]
+                    remote(
+                        passing.at[j, i], target, q_send.at[r, j, i], o_recv, last, to_t
+                    ).start()
+
+            @pl.loop(0, owned)
+            def _(j):
+                for i in range(far):
+                    arrived(passing.at[j, i], q_send.at[r, j, i])
+
     arrived(out, o_recv)
 
     @pl.loop(0, owned)
     def _(j):
         for i, to_t in enumerate(peers):
             arrived(tokens.at[:, lane(to_t * owned + j, width)], t_send.at[j, i])
-            arrived(xout.at[j, lane(to_t, rows)], o_send.at[j, i])
+
+            @pl.when(g < last)
+            def _():
+                arrived(xout.at[j, lane(to_t, rows)], o_send.at[j, i])
+
+        @pl.when(g == last)
+        def _():
+            for i in range(far):
+                arrived(xout.at[j, :kept], o_send.at[j, i])
+                for r in range(2):
+                    arrived(passing.at[j, i], q_send.at[r, j, i])
+            arrived(xout.at[j, :rows], o_send.at[j, far])
 
         @pl.when(g < last)
         def _():
@@ -470,19 +556,21 @@
     layers, _, owned, width, _ = fast_init.shape
     rows, channels = tokens.shape
     group_tok = rows * toks
+    gains = channel_gains.transpose(1, 0, 2)
     sizes = (groups, toks, layers, owned, rows, width, TILE)
-    smem = pl.BlockSpec(memory_space=pltpu.SMEM)
     anywhere = pl.BlockSpec(memory_space=pl.ANY)
     dma = pltpu.SemaphoreType.DMA
     return pl.pallas_call(
         functools.partial(wave_kernel, sizes),
         out_shape=jax.ShapeDtypeStruct((rows, channels), BF16),
-        in_specs=[smem, smem, anywhere, anywhere, anywhere, anywhere],
+        in_specs=[anywhere] * 6,
         out_specs=anywhere,
         scratch_shapes=[
+            pltpu.SMEM(step_size.shape, F32),
+            pltpu.SMEM(update_table.shape, jnp.int32),
             pltpu.VMEM(tokens.shape, BF16),
             pltpu.VMEM(learning_rates.shape, F32),
-            pltpu.VMEM(channel_gains.shape, F32),
+            pltpu.VMEM(gains.shape, F32),
             pltpu.VMEM(fast_init.shape, F32),
             pltpu.VMEM((layers, owned, group_tok, width), BF16),
             pltpu.VMEM((owned, group_tok, width), BF16),
@@ -505,22 +593,26 @@
             dma((layers, owned)),
             dma((owned, toks)),
             dma,
-            dma((4,)),
+            dma((6,)),
+            pltpu.VMEM((owned, toks - 2, rows // 64 * 16, width), BF16),
+            dma((2, owned, toks - 2)),
+            dma((owned, toks - 2)),
         ],
         compiler_params=pltpu.CompilerParams(
-            collective_id=0, has_side_effects=True, vmem_limit_bytes=48 * 1024 * 1024
+            collective_id=0, has_side_effects=True, vmem_limit_bytes=VMEM_LIMIT
         ),
-    )(step_size, update_table, tokens, learning_rates, channel_gains, fast_init)
+    )(step_size, update_table, tokens, learning_rates, gains, fast_init)
 
 
 TILE = 2048
+VMEM_LIMIT = 67_043_328
 
 
 def plan(mesh, tokens, fast_init):
     groups, toks = mesh.shape["group"], mesh.shape["tok"]
     layers, _, heads, width, _ = fast_init.shape
     rows = tokens.shape[0] // (groups * toks)
-    fits = groups > 1 and toks > 2 and toks % 2 == 0 and layers > 1 and heads % toks == 0
+    fits = groups > 4 and toks > 2 and toks % 2 == 0 and layers > 1 and heads % toks == 0
     fits = fits and rows * toks % TILE == 0 and rows % 128 == 0 and width % 128 == 0
     return wave_body if fits and tokens.shape[0] * tokens.shape[1] <= 64 * 1024 * 1024 else body
 

time: 131 us -> 128 us (0.977)
  local copies, waits for them, and re-layouts: 7.12 us -> 3.16 us
    unnamed x12 -> x1, local copies, waits for them, and re-layouts: 7.12 us -> 3.16 us
where the time goes in v3:
time: 128 us
  Pallas kernels  124 us (97%)
  local copies, waits for them, and re-layouts  3.16 us (2%)
    pallas_call x1, Pallas kernels, wave_body(): pl.pallas_call(functools.partial(wave_kernel, sizes), out_shape=jax.Shape...  124 us
    unnamed x1, local copies, waits for them, and re-layouts  3.16 us

profile of v3, /device:TPU:25, one launch (start us, length us, event | category | flops | bytes accessed | tf_op | source)
XLA Modules:
  0.0 127.6 jit_solution(10598898510566372296)
XLA Ops:
  0.0 124.5 %shard_map.64 = bf16[512,2048]{1,0:T(8,128)(2,1)} custom-call(f32[2,4]{1,0:T(2,128)} %steps_in.1, s32[2,8]{1,0:T(2,128)} %table_in.1, bf16[512,2048]{1,0:T(8,128)(2,1)} %tokens_in.1, f32[2,2048]{1,0:T(2,128)} %rates_in.1, f32[5,2,512]{2,1,0:T(2,128)} %bitcast.1, f32[2,3,4,128,128]{4,3,2,1,0:T(8,128)} %initial_in.1), custom_call_target="tpu_custom_call" | custom-call | tf_op jit(solution)/shard_map/pallas_call | solution.py:563
  124.5 3.2 %copy.8 = bf16[512,2048]{1,0:T(8,128)(2,1)} copy(bf16[512,2048]{1,0:T(8,128)(2,1)} %shard_map.64) | data formatting | bytes 4194304

commit v4 on v3

--- a/solution.py
+++ b/solution.py
@@ -271,9 +271,10 @@
         for to_t in peers[:far]:
             greet(near_g, to_t)
     pl.semaphore_wait(barrier, toks + 3 + 2 * far)
-    relays = (groups - 3, 1)
-    share = rows // 64 * 16
-    kept = rows - 2 * share
+    share = passing.shape[2]
+    kept = rows - share
+    late = g >= groups - 2
+    at_once = owned // 2
 
     def hand_out(j):
         target = xin.at[0, j, lane(t, rows)]
@@ -363,26 +364,25 @@
         if l == layers - 1:
             target = out.at[:, lane(t * owned + j, width)]
 
-            @pl.when(g < last)
+            @pl.when(jnp.logical_not(late))
             def _():
-                for i, to_t in enumerate(peers):
+                for i, to_t in enumerate(peers[:far]):
                     source = xout.at[j, lane(to_t, rows)]
                     remote(source, target, o_send.at[j, i], o_recv, g, to_t).start()
 
-            @pl.when(g == last)
+            @pl.when(late)
             def _():
                 for i, to_t in enumerate(peers[:far]):
-                    for r, relay in enumerate(relays):
-                        source = xout.at[j, pl.ds(to_t * rows + kept + r * share, share)]
-                        remote(
-                            source, passing.at[j, i], q_send.at[r, j, i], q_recv.at[j, i], relay, t
-                        ).start()
-                for i, to_t in enumerate(peers[:far]):
+                    source = xout.at[j, pl.ds(to_t * rows + kept, share)]
+                    relay = g + 2 - groups
+                    remote(
+                        source, passing.at[j, i], q_send.at[j, i], q_recv.at[j, i], relay, t
+                    ).start()
                     source = xout.at[j, pl.ds(to_t * rows, kept)]
                     remote(source, target.at[:kept], o_send.at[j, i], o_recv, g, to_t).start()
-                source = xout.at[j, lane(peers[far], rows)]
-                remote(source, target, o_send.at[j, far], o_recv, g, peers[far]).start()
-
+
+            source = xout.at[j, lane(peers[far], rows)]
+            remote(source, target, o_send.at[j, far], o_recv, g, peers[far]).start()
             pltpu.make_async_copy(xout.at[j, lane(t, rows)], target, o_recv).start()
 
     def learn(l, j):
@@ -493,33 +493,31 @@
             def _(j):
                 chain(l, j)
 
-                @pl.when(g == last)
+                @pl.when(jnp.logical_or(g == last, jnp.logical_and(g >= groups // 2, j < at_once)))
                 def _():
                     query(l, j)
 
             @pl.when(g < last)
             def _():
-                @pl.loop(0, owned)
+                @pl.loop(jnp.where(g >= groups // 2, at_once, 0), owned)
                 def _(j):
                     query(l, j)
 
-    for r, relay in enumerate(relays):
-
-        @pl.when(g == relay)
-        def _():
-            @pl.loop(0, owned)
-            def _(j):
-                for i, to_t in enumerate(peers[:far]):
-                    arrived(passing.at[j, i], q_recv.at[j, i])
-                    target = out.at[pl.ds(kept + r * share, share), lane(t * owned + j, width)]
-                    remote(
-                        passing.at[j, i], target, q_send.at[r, j, i], o_recv, last, to_t
-                    ).start()
-
-            @pl.loop(0, owned)
-            def _(j):
-                for i in range(far):
-                    arrived(passing.at[j, i], q_send.at[r, j, i])
+    @pl.when(g < 2)
+    def _():
+        @pl.loop(0, owned)
+        def _(j):
+            for i, to_t in enumerate(peers[:far]):
+                arrived(passing.at[j, i], q_recv.at[j, i])
+                target = out.at[pl.ds(kept, share), lane(t * owned + j, width)]
+                remote(
+                    passing.at[j, i], target, q_send.at[j, i], o_recv, g + groups - 2, to_t
+                ).start()
+
+        @pl.loop(0, owned)
+        def _(j):
+            for i in range(far):
+                arrived(passing.at[j, i], q_send.at[j, i])
 
     arrived(out, o_recv)
 
@@ -527,18 +525,18 @@
     def _(j):
         for i, to_t in enumerate(peers):
             arrived(tokens.at[:, lane(to_t * owned + j, width)], t_send.at[j, i])
-
-            @pl.when(g < last)
-            def _():
-                arrived(xout.at[j, lane(to_t, rows)], o_send.at[j, i])
-
-        @pl.when(g == last)
+        arrived(xout.at[j, :rows], o_send.at[j, far])
+
+        @pl.when(jnp.logical_not(late))
+        def _():
+            for i in range(far):
+                arrived(xout.at[j, :rows], o_send.at[j, i])
+
+        @pl.when(late)
         def _():
             for i in range(far):
                 arrived(xout.at[j, :kept], o_send.at[j, i])
-                for r in range(2):
-                    arrived(passing.at[j, i], q_send.at[r, j, i])
-            arrived(xout.at[j, :rows], o_send.at[j, far])
+                arrived(passing.at[j, i], q_send.at[j, i])
 
         @pl.when(g < last)
         def _():
@@ -594,8 +592,8 @@
             dma((owned, toks)),
             dma,
             dma((6,)),
-            pltpu.VMEM((owned, toks - 2, rows // 64 * 16, width), BF16),
-            dma((2, owned, toks - 2)),
+            pltpu.VMEM((owned, toks - 2, rows // 256 * 80, width), BF16),
+            dma((owned, toks - 2)),
             dma((owned, toks - 2)),
         ],
         compiler_params=pltpu.CompilerParams(
@@ -613,7 +611,7 @@
     layers, _, heads, width, _ = fast_init.shape
     rows = tokens.shape[0] // (groups * toks)
     fits = groups > 4 and toks > 2 and toks % 2 == 0 and layers > 1 and heads % toks == 0
-    fits = fits and rows * toks % TILE == 0 and rows % 128 == 0 and width % 128 == 0
+    fits = fits and rows * toks % TILE == 0 and rows % 256 == 0 and width % 128 == 0
     return wave_body if fits and tokens.shape[0] * tokens.shape[1] <= 64 * 1024 * 1024 else body
 
 

time: 128 us -> 121 us (0.945)
  the two profiles are of different devices: /device:TPU:25 before, /device:TPU:29 now
where the time goes in v4:
time: 121 us
  Pallas kernels  117 us (97%)
  local copies, waits for them, and re-layouts  3.16 us (3%)
    pallas_call x1, Pallas kernels, wave_body(): pl.pallas_call(functools.partial(wave_kernel, sizes), out_shape=jax.Shape...  117 us
    unnamed x1, local copies, waits for them, and re-layouts  3.16 us

profile of v4, /device:TPU:29, one launch (start us, length us, event | category | flops | bytes accessed | tf_op | source)
XLA Modules:
  0.0 120.6 jit_solution(9466599946391084963)
XLA Ops:
  0.0 117.5 %shard_map.64 = bf16[512,2048]{1,0:T(8,128)(2,1)} custom-call(f32[2,4]{1,0:T(2,128)} %steps_in.1, s32[2,8]{1,0:T(2,128)} %table_in.1, bf16[512,2048]{1,0:T(8,128)(2,1)} %tokens_in.1, f32[2,2048]{1,0:T(2,128)} %rates_in.1, f32[5,2,512]{2,1,0:T(2,128)} %bitcast.1, f32[2,3,4,128,128]{4,3,2,1,0:T(8,128)} %initial_in.1), custom_call_target="tpu_custom_call" | custom-call | tf_op jit(solution)/shard_map/pallas_call | solution.py:561
  117.5 3.2 %copy.8 = bf16[512,2048]{1,0:T(8,128)(2,1)} copy(bf16[512,2048]{1,0:T(8,128)(2,1)} %shard_map.64) | data formatting | bytes 4194304

commit v5 on v4

--- a/solution.py
+++ b/solution.py
@@ -190,7 +190,7 @@
     squares,
     partial,
     partials,
-    stack,
+    scales,
     grad_gu,
     grad_d,
     t_send,
@@ -326,15 +326,16 @@
 
     def scale_rows(l, at, sums):
         size = sums.shape[1]
+        at_row = lax.broadcasted_iota(jnp.int32, (16, size), 0)
         inverse = lax.rsqrt(sums / (owned * toks * width) + EPSILON)
-        rate = rates[l : l + 1, at]
+        rated = inverse * rates[l : l + 1, at]
         inverse_high = inverse.astype(BF16).astype(F32)
-        rate_high = rate.astype(BF16).astype(F32)
-        at_row = lax.broadcasted_iota(jnp.int32, (16, size), 0)
+        rated_high = rated.astype(BF16).astype(F32)
         fill = jnp.where(at_row == 0, inverse_high, 0.0)
         fill = jnp.where(at_row == 1, inverse - inverse_high, fill)
-        fill = jnp.where(at_row == 2, rate_high, fill)
-        stack[:, at] = jnp.where(at_row == 3, rate - rate_high, fill).astype(BF16)
+        fill = jnp.where(at_row == 2, rated_high, fill)
+        fill = jnp.where(at_row == 3, rated - rated_high, fill)
+        scales[at, :] = dot(fill.astype(BF16), spread, TN)
 
     def gains_of(l, j):
         rows_of = gains[:, l, lane(j, width)]
@@ -345,12 +346,10 @@
         query_gain, _, _, out_gain = gains_of(l, j)
         size = min(tile, group_tok)
 
-        @pl.loop(0, group_tok // size)
-        def _(i):
+        def answer(i):
             here = lane(i, size)
             stream = xin[l, j, here, :].astype(F32)
-            normed = stream * dot(stack[:, here], spread[:, :width], TN)
-            queries = (normed * query_gain).astype(BF16)
+            queries = (stream * scales[here, :width] * query_gain).astype(BF16)
             both = dot(queries, weights[l, j, :, : 2 * width])
             gate = both[:, :width]
             hidden = (gate * sigmoid(gate) * both[:, width:]).astype(BF16)
@@ -361,29 +360,34 @@
             else:
                 xout[j, here, :] = mixed
 
-        if l == layers - 1:
-            target = out.at[:, lane(t * owned + j, width)]
-
-            @pl.when(jnp.logical_not(late))
-            def _():
-                for i, to_t in enumerate(peers[:far]):
-                    source = xout.at[j, lane(to_t, rows)]
-                    remote(source, target, o_send.at[j, i], o_recv, g, to_t).start()
-
-            @pl.when(late)
-            def _():
-                for i, to_t in enumerate(peers[:far]):
-                    source = xout.at[j, pl.ds(to_t * rows + kept, share)]
-                    relay = g + 2 - groups
-                    remote(
-                        source, passing.at[j, i], q_send.at[j, i], q_recv.at[j, i], relay, t
-                    ).start()
-                    source = xout.at[j, pl.ds(to_t * rows, kept)]
-                    remote(source, target.at[:kept], o_send.at[j, i], o_recv, g, to_t).start()
-
-            source = xout.at[j, lane(peers[far], rows)]
-            remote(source, target, o_send.at[j, far], o_recv, g, peers[far]).start()
-            pltpu.make_async_copy(xout.at[j, lane(t, rows)], target, o_recv).start()
+        if size == group_tok:
+            answer(0)
+        else:
+            pl.loop(0, group_tok // size)(answer)
+
+    def send_home(j):
+        target = out.at[:, lane(t * owned + j, width)]
+
+        @pl.when(jnp.logical_not(late))
+        def _():
+            for i, to_t in enumerate(peers[:far]):
+                source = xout.at[j, lane(to_t, rows)]
+                remote(source, target, o_send.at[j, i], o_recv, g, to_t).start()
+
+        @pl.when(late)
+        def _():
+            for i, to_t in enumerate(peers[:far]):
+                source = xout.at[j, pl.ds(to_t * rows + kept, share)]
+                relay = g + 2 - groups
+                remote(
+                    source, passing.at[j, i], q_send.at[j, i], q_recv.at[j, i], relay, t
+                ).start()
+                source = xout.at[j, pl.ds(to_t * rows, kept)]
+                remote(source, target.at[:kept], o_send.at[j, i], o_recv, g, to_t).start()
+
+        source = xout.at[j, lane(peers[far], rows)]
+        remote(source, target, o_send.at[j, far], o_recv, g, peers[far]).start()
+        pltpu.make_async_copy(xout.at[j, lane(t, rows)], target, o_recv).start()
 
     def learn(l, j):
         _, key_gain, value_gain, _ = gains_of(l, j)
@@ -391,10 +395,9 @@
 
         def found(i):
             here = lane(i, size)
-            scale = dot(stack[:, here], spread, TN)
-            normed = xin[l, j, here, :].astype(F32) * scale[:, :width]
-            keys = (normed * key_gain).astype(BF16)
-            targets = (normed * value_gain * scale[:, width:]).astype(BF16)
+            stream = xin[l, j, here, :].astype(F32)
+            keys = (stream * scales[here, :width] * key_gain).astype(BF16)
+            targets = (stream * scales[here, width:] * value_gain).astype(BF16)
             both = dot(keys, weights[l, j, :, : 2 * width])
             back = dot(targets, weights[l, j, :, 2 * width :], NT)
             gate = both[:, :width]
@@ -420,14 +423,14 @@
 
         return grad_gu[...], grad_d[...]
 
-    def chain(l, j):
+    def chain(l, j, asked=False):
         @pl.when(g > 0)
         def _():
             arrived(weights.at[l, j], w_recv.at[l, j])
 
-        chain_go(l, j)
-
-    def chain_go(l, j):
+        chain_go(l, j, asked)
+
+    def chain_go(l, j, asked=False):
         @pl.when(g < last)
         def _():
             both, below = learn(l, j)
@@ -437,6 +440,8 @@
             )
             for repeat in range(NS_STEPS):
                 moves = newton_schulz(moves, coarse if repeat < 2 else product)
+            if asked:
+                query(l, j)
             step = steps[l, j] * table[l, g].astype(F32)
             for which in range(3):
                 at = slice(which * width, (which + 1) * width)
@@ -472,8 +477,11 @@
             def _(j):
                 if l == 0:
                     await_tokens(j)
-                chain(l, j)
-                query(l, j)
+                chain(l, j, True)
+
+                @pl.when(g == last)
+                def _():
+                    query(l, j)
 
             if l == 0:
                 await_tokens(owned - 1)
@@ -496,12 +504,14 @@
                 @pl.when(jnp.logical_or(g == last, jnp.logical_and(g >= groups // 2, j < at_once)))
                 def _():
                     query(l, j)
+                    send_home(j)
 
             @pl.when(g < last)
             def _():
                 @pl.loop(jnp.where(g >= groups // 2, at_once, 0), owned)
                 def _(j):
                     query(l, j)
+                    send_home(j)
 
     @pl.when(g < 2)
     def _():
@@ -578,7 +588,7 @@
             pltpu.VMEM((toks, 1, rows), F32),
             pltpu.VMEM((layers - 1, 1, group_tok), F32),
             pltpu.VMEM((layers - 1, toks, 1, group_tok), F32),
-            pltpu.VMEM((16, group_tok), BF16),
+            pltpu.VMEM((group_tok, 2 * width), F32),
             pltpu.VMEM((width, 2 * width), F32),
             pltpu.VMEM((width, width), F32),
             dma((owned, toks)),

time: 121 us -> 118 us (0.975)
  Pallas kernels: 117 us -> 115 us
    pallas_call x1, Pallas kernels: 117 us -> 115 us  [wave_body(): pl.pallas_call(functools.partial(wave_kernel, sizes), out_shape=jax.Shape...]
where the time goes in v5:
time: 118 us
  Pallas kernels  115 us (97%)
  local copies, waits for them, and re-layouts  3.16 us (3%)
    pallas_call x1, Pallas kernels, wave_body(): pl.pallas_call(functools.partial(wave_kernel, sizes), out_shape=jax.Shape...  115 us
    unnamed x1, local copies, waits for them, and re-layouts  3.16 us

profile of v5, /device:TPU:29, one launch (start us, length us, event | category | flops | bytes accessed | tf_op | source)
XLA Modules:
  0.0 118.3 jit_solution(3267776480615230153)
XLA Ops:
  0.0 115.2 %shard_map.64 = bf16[512,2048]{1,0:T(8,128)(2,1)} custom-call(f32[2,4]{1,0:T(2,128)} %steps_in.1, s32[2,8]{1,0:T(2,128)} %table_in.1, bf16[512,2048]{1,0:T(8,128)(2,1)} %tokens_in.1, f32[2,2048]{1,0:T(2,128)} %rates_in.1, f32[5,2,512]{2,1,0:T(2,128)} %bitcast.1, f32[2,3,4,128,128]{4,3,2,1,0:T(8,128)} %initial_in.1), custom_call_target="tpu_custom_call" | custom-call | tf_op jit(solution)/shard_map/pallas_call | solution.py:571
  115.2 3.2 %copy.8 = bf16[512,2048]{1,0:T(8,128)(2,1)} copy(bf16[512,2048]{1,0:T(8,128)(2,1)} %shard_map.64) | data formatting | bytes 4194304

commit v6 on v5

--- a/solution.py
+++ b/solution.py
@@ -204,6 +204,7 @@
     o_send,
     o_recv,
     i_recv,
+    l_recv,
     passing,
     q_send,
     q_recv,
@@ -234,7 +235,6 @@
         pltpu.make_async_copy(source, target, i_recv.at[i])
         for i, (source, target) in enumerate(
             [
-                (tokens_in, tokens),
                 (rates_in, rates),
                 (gains_in, gains),
                 (steps_in, steps),
@@ -243,12 +243,20 @@
             ]
         )
     ]
-    for load in loads[:5]:
+    for load in loads[:4]:
         load.start()
+
+    @pl.loop(0, owned)
+    def _(j):
+        for to_t in range(toks):
+            h = to_t * owned + j
+            pltpu.make_async_copy(
+                tokens_in.at[:, lane(h, width)], tokens.at[h], l_recv.at[j]
+            ).start()
 
     @pl.when(g == 0)
     def _():
-        loads[5].start()
+        loads[4].start()
 
     barrier = pltpu.get_barrier_semaphore()
 
@@ -279,12 +287,12 @@
     def hand_out(j):
         target = xin.at[0, j, lane(t, rows)]
         for i, to_t in enumerate(peers):
-            source = tokens.at[:, lane(to_t * owned + j, width)]
+            source = tokens.at[to_t * owned + j]
             remote(source, target, t_send.at[j, i], t_recv.at[j, t], g, to_t).start()
-        source = tokens.at[:, lane(t * owned + j, width)]
+        source = tokens.at[t * owned + j]
         pltpu.make_async_copy(source, target, t_recv.at[j, t]).start()
 
-    loads[0].wait()
+    arrived(tokens.at[:toks], l_recv.at[0])
     hand_out(0)
     ones_rows = jnp.ones((16, width), BF16)
 
@@ -292,11 +300,19 @@
         wide = values.astype(F32)
         return dot(ones_rows, (wide * wide).astype(BF16), NT)[0:1]
 
-    totals[...] = jnp.zeros_like(totals)
-
-    @pl.loop(0, owned * toks)
-    def _(h):
-        totals[...] += sums_of(tokens[:, lane(h, width)])
+    for j in range(1, owned):
+        arrived(tokens.at[:toks], l_recv.at[j])
+
+    @pl.loop(0, rows // 128)
+    def _(i):
+        here = lane(i, 128)
+        tally = jnp.zeros((128, width), F32)
+        for h in range(owned * toks):
+            wide = tokens[h, here, :].astype(F32)
+            tally += wide * wide
+        high = tally.astype(BF16)
+        low = (tally - high.astype(F32)).astype(BF16)
+        totals[:, here] = (dot(ones_rows, high, NT) + dot(ones_rows, low, NT))[0:1]
 
     squares[t] = totals[...]
     for i, to_t in enumerate(peers):
@@ -306,12 +322,12 @@
     def _(j):
         hand_out(j)
 
-    for load in loads[1:5]:
+    for load in loads[:4]:
         load.wait()
 
     @pl.when(g == 0)
     def _():
-        loads[5].wait()
+        loads[4].wait()
         for l in range(layers):
             @pl.loop(0, owned)
             def _(j):
@@ -534,7 +550,7 @@
     @pl.loop(0, owned)
     def _(j):
         for i, to_t in enumerate(peers):
-            arrived(tokens.at[:, lane(to_t * owned + j, width)], t_send.at[j, i])
+            arrived(tokens.at[to_t * owned + j], t_send.at[j, i])
         arrived(xout.at[j, :rows], o_send.at[j, far])
 
         @pl.when(jnp.logical_not(late))
@@ -566,6 +582,7 @@
     group_tok = rows * toks
     gains = channel_gains.transpose(1, 0, 2)
     sizes = (groups, toks, layers, owned, rows, width, TILE)
+    pin = lambda x: pltpu.with_memory_space_constraint(x, pltpu.HBM)
     anywhere = pl.BlockSpec(memory_space=pl.ANY)
     dma = pltpu.SemaphoreType.DMA
     return pl.pallas_call(
@@ -576,7 +593,7 @@
         scratch_shapes=[
             pltpu.SMEM(step_size.shape, F32),
             pltpu.SMEM(update_table.shape, jnp.int32),
-            pltpu.VMEM(tokens.shape, BF16),
+            pltpu.VMEM((channels // width, rows, width), BF16),
             pltpu.VMEM(learning_rates.shape, F32),
             pltpu.VMEM(gains.shape, F32),
             pltpu.VMEM(fast_init.shape, F32),
@@ -601,7 +618,8 @@
             dma((layers, owned)),
             dma((owned, toks)),
             dma,
-            dma((6,)),
+            dma((5,)),
+            dma((owned,)),
             pltpu.VMEM((owned, toks - 2, rows // 256 * 80, width), BF16),
             dma((owned, toks - 2)),
             dma((owned, toks - 2)),
@@ -609,11 +627,11 @@
         compiler_params=pltpu.CompilerParams(
             collective_id=0, has_side_effects=True, vmem_limit_bytes=VMEM_LIMIT
         ),
-    )(step_size, update_table, tokens, learning_rates, gains, fast_init)
+    )(*map(pin, (step_size, update_table, tokens, learning_rates, gains, fast_init)))
 
 
 TILE = 2048
-VMEM_LIMIT = 67_043_328
+VMEM_LIMIT = 50 * 1024 * 1024
 
 
 def plan(mesh, tokens, fast_init):

time: 118 us -> 117 us (level)
  local copies, waits for them, and re-layouts: 3.16 us -> 1.32 us
    unnamed x1, local copies, waits for them, and re-layouts: 3.16 us -> 1.32 us
where the time goes in v6:
time: 117 us; the launch traced here: 116 us
  Pallas kernels  115 us (98%)
  local copies, waits for them, and re-layouts  1.32 us (1%)
    pallas_call x1, Pallas kernels, wave_body(): pl.pallas_call(functools.partial(wave_kernel, sizes), out_shape=jax.Shape...  115 us

profile of v6, /device:TPU:29, one launch (start us, length us, event | category | flops | bytes accessed | tf_op | source)
XLA Modules:
  0.0 116.5 jit_solution(8305044228627359949)
XLA Ops:
  0.0 115.2 %shard_map.64 = bf16[512,2048]{1,0:T(8,128)(2,1)S(1)} custom-call(f32[2,4]{1,0:T(2,128)} %steps_in.1, s32[2,8]{1,0:T(2,128)} %table_in.1, bf16[512,2048]{1,0:T(8,128)(2,1)} %tokens_in.1, f32[2,2048]{1,0:T(2,128)} %rates_in.1, f32[5,2,512]{2,1,0:T(2,128)} %bitcast.1, f32[2,3,4,128,128]{4,3,2,1,0:T(8,128)} %initial_in.1), custom_call_target="tpu_custom_call" | custom-call | tf_op jit(solution)/shard_map/pallas_call | solution.py:588
  115.2 1.3 %copy.8 = bf16[512,2048]{1,0:T(8,128)(2,1)} copy(bf16[512,2048]{1,0:T(8,128)(2,1)S(1)} %shard_map.64) | data formatting | bytes 4194304

commit v7 on v6

--- a/solution.py
+++ b/solution.py
@@ -158,6 +158,20 @@
 
 def coarse(a, b):
     return dot(a.astype(BF16), b.astype(BF16))
+
+
+def first_step(values):
+    rounded = [v.astype(BF16) for v in values]
+    squares = [dot(v, v, NT) for v in rounded]
+    scales = [
+        lax.rsqrt(jnp.sum(v * v, axis=(0, 1), keepdims=True) + EPSILON) for v in values
+    ]
+    squares = [q * (r * r) for q, r in zip(squares, scales)]
+    polynoms = [MUON_B * q + MUON_C * coarse(q, q) for q in squares]
+    return tuple(
+        r * (MUON_A * v + dot(p.astype(BF16), n))
+        for p, v, n, r in zip(polynoms, values, rounded, scales)
+    )
 
 
 def newton_schulz(values, times):
@@ -243,21 +257,6 @@
             ]
         )
     ]
-    for load in loads[:4]:
-        load.start()
-
-    @pl.loop(0, owned)
-    def _(j):
-        for to_t in range(toks):
-            h = to_t * owned + j
-            pltpu.make_async_copy(
-                tokens_in.at[:, lane(h, width)], tokens.at[h], l_recv.at[j]
-            ).start()
-
-    @pl.when(g == 0)
-    def _():
-        loads[4].start()
-
     barrier = pltpu.get_barrier_semaphore()
 
     def greet(to_g, to_t):
@@ -278,6 +277,21 @@
         greet(near_g, t)
         for to_t in peers[:far]:
             greet(near_g, to_t)
+    for load in loads[:4]:
+        load.start()
+
+    @pl.loop(0, owned)
+    def _(j):
+        for to_t in range(toks):
+            h = to_t * owned + j
+            pltpu.make_async_copy(
+                tokens_in.at[:, lane(h, width)], tokens.at[h], l_recv.at[j]
+            ).start()
+
+    @pl.when(g == 0)
+    def _():
+        loads[4].start()
+
     pl.semaphore_wait(barrier, toks + 3 + 2 * far)
     share = passing.shape[2]
     kept = rows - share
@@ -451,10 +465,8 @@
         def _():
             both, below = learn(l, j)
             grads = (both[:, :width], both[:, width:], below)
-            moves = tuple(
-                v * lax.rsqrt(jnp.sum(v * v, axis=(0, 1), keepdims=True) + EPSILON) for v in grads
-            )
-            for repeat in range(NS_STEPS):
+            moves = first_step(grads)
+            for repeat in range(1, NS_STEPS):
                 moves = newton_schulz(moves, coarse if repeat < 2 else product)
             if asked:
                 query(l, j)

time: 117 us -> 116 us (level)
  no operation moved by 1% of the time
where the time goes in v7:
time: 116 us; the launch traced here: 115 us
  Pallas kernels  114 us (98%)
  local copies, waits for them, and re-layouts  1.32 us (1%)
    pallas_call x1, Pallas kernels, wave_body(): pl.pallas_call(functools.partial(wave_kernel, sizes), out_shape=jax.Shape...  114 us

profile of v7, /device:TPU:29, one launch (start us, length us, event | category | flops | bytes accessed | tf_op | source)
XLA Modules:
  0.0 115.4 jit_solution(18414585118283477908)
XLA Ops:
  0.0 114.1 %shard_map.64 = bf16[512,2048]{1,0:T(8,128)(2,1)S(1)} custom-call(f32[2,4]{1,0:T(2,128)} %steps_in.1, s32[2,8]{1,0:T(2,128)} %table_in.1, bf16[512,2048]{1,0:T(8,128)(2,1)} %tokens_in.1, f32[2,2048]{1,0:T(2,128)} %rates_in.1, f32[5,2,512]{2,1,0:T(2,128)} %bitcast.1, f32[2,3,4,128,128]{4,3,2,1,0:T(8,128)} %initial_in.1), custom_call_target="tpu_custom_call" | custom-call | tf_op jit(solution)/shard_map/pallas_call | solution.py:600
  114.1 1.3 %copy.8 = bf16[512,2048]{1,0:T(8,128)(2,1)} copy(bf16[512,2048]{1,0:T(8,128)(2,1)S(1)} %shard_map.64) | data formatting | bytes 4194304

commit v8 on v7

--- a/solution.py
+++ b/solution.py
@@ -527,12 +527,21 @@
         else:
             @pl.loop(0, owned)
             def _(j):
-                chain(l, j)
-
-                @pl.when(jnp.logical_or(g == last, jnp.logical_and(g >= groups // 2, j < at_once)))
+                here = jnp.logical_and(g >= groups // 2, jnp.logical_or(g == last, j < at_once))
+
+                @pl.when(here)
                 def _():
-                    query(l, j)
+                    chain(l, j, True)
+
+                    @pl.when(g == last)
+                    def _():
+                        query(l, j)
+
                     send_home(j)
+
+                @pl.when(jnp.logical_not(here))
+                def _():
+                    chain(l, j)
 
             @pl.when(g < last)
             def _():

time: 116 us -> 116 us (level)
  no operation moved by 1% of the time
where the time goes in v8:
time: 116 us
  Pallas kernels  114 us (98%)
  local copies, waits for them, and re-layouts  1.32 us (1%)
    pallas_call x1, Pallas kernels, wave_body(): pl.pallas_call(functools.partial(wave_kernel, sizes), out_shape=jax.Shape...  114 us

profile of v8, /device:TPU:29, one launch (start us, length us, event | category | flops | bytes accessed | tf_op | source)
XLA Modules:
  0.0 115.5 jit_solution(14087721917504441283)
XLA Ops:
  0.0 114.2 %shard_map.64 = bf16[512,2048]{1,0:T(8,128)(2,1)S(1)} custom-call(f32[2,4]{1,0:T(2,128)} %steps_in.1, s32[2,8]{1,0:T(2,128)} %table_in.1, bf16[512,2048]{1,0:T(8,128)(2,1)} %tokens_in.1, f32[2,2048]{1,0:T(2,128)} %rates_in.1, f32[5,2,512]{2,1,0:T(2,128)} %bitcast.1, f32[2,3,4,128,128]{4,3,2,1,0:T(8,128)} %initial_in.1), custom_call_target="tpu_custom_call" | custom-call | tf_op jit(solution)/shard_map/pallas_call | solution.py:609
  114.2 1.3 %copy.8 = bf16[512,2048]{1,0:T(8,128)(2,1)} copy(bf16[512,2048]{1,0:T(8,128)(2,1)S(1)} %shard_map.64) | data formatting | bytes 4194304
